TPU v7x, 64 devices: a 2x2x8 block of a 4x4x8 slice. The times are simulated.
64 devices in a mesh: dp: 4 (over x, y), tp: 16 (over z, core).
Axes of the slice: x: 2, y: 2, z: 8, core: 2. Of those that a mesh axis runs over, the one named last changes fastest.
The devices are a block of a 4x4x8 slice.
Arguments:
- x_tokens: bfloat16 [4, 4096, 1536], P('dp', 'tp'), parts along dimension 0
- ln1_gain: float32 [2, 1536], replicated
- ln1_bias: float32 [2, 1536], replicated
- ln2_gain: float32 [2, 1536], replicated
- ln2_bias: float32 [2, 1536], replicated
- w_qkv: bfloat16 [2, 1536, 3, 16, 96], P(None, None, None, 'tp')
- w_out: bfloat16 [2, 16, 96, 1536], P(None, 'tp')
- b_out: float32 [2, 1536], replicated
- w_up: bfloat16 [2, 1536, 6144], P(None, None, 'tp')
- b_up: float32 [2, 6144], P(None, 'tp')
- w_down: bfloat16 [2, 6144, 1536], P(None, 'tp')
- b_down: float32 [2, 1536], replicated
Outputs:
- output: bfloat16 [4, 4096, 1536], P('dp', 'tp'), parts along dimension 0
There are 4 independent parts. A program takes and returns all parts, laid end to end along the dimension named above; an argument that names none is the same for every part.
All inputs are finite; a program needn't handle non-finite values.
Results may differ from a plain program's by a relative error of at most 0.010894.
Values are sent between devices in bfloat16 or wider.
A program may use at most 768 MiB of HBM per device.

v0:
```python
import functools
import math
import jax
import jax.numpy as jnp
from jax import lax
from jax.experimental import pallas as pl
from jax.experimental.pallas import tpu as pltpu
from jax.sharding import PartitionSpec as P

BF16, F32 = jnp.bfloat16, jnp.float32
LANES = 128


def layer_norm(resid, gain, shift):
    row_mean = jnp.mean(resid, axis=-1, keepdims=True)
    centered = resid - row_mean
    variance = jnp.mean(centered * centered, axis=-1, keepdims=True)
    return (centered * lax.rsqrt(variance + 1e-5) * gain + shift).astype(BF16)


def attention_kernel(scale, part, share, head_dim, h_ref, w_ref, o_ref, k_scr, v_scr):
    i = pl.program_id(0)
    rows = k_scr.shape[0] // pl.num_programs(0)
    here = pl.ds(pl.multiple_of(i * rows, rows), rows)
    hidden = h_ref[...].reshape(rows, h_ref.shape[-1])
    qkv = jnp.dot(hidden, w_ref[...], preferred_element_type=F32).astype(BF16)
    q, k, v = (qkv[:, n * LANES : (n + 1) * LANES] for n in range(3))
    k_scr[here, :] = k
    v_scr[here, :] = v
    to_exp2 = scale * math.log2(math.e)
    queries = [q[n * part : (n + 1) * part] for n in range(rows // part)]

    def scores(keys, query):
        return lax.dot_general(keys, query, (((1,), (1,)), ((), ())), preferred_element_type=F32) * to_exp2

    def weighted(values, probs):
        return lax.dot_general(values, probs, (((0,), (0,)), ((), ())), preferred_element_type=F32)

    state = []
    for n, query in enumerate(queries):
        seen = (n + 1) * part
        s = scores(k[:seen], query)
        key_at = lax.broadcasted_iota(jnp.int32, s.shape, 0)
        query_at = lax.broadcasted_iota(jnp.int32, s.shape, 1) + n * part
        s = jnp.where(key_at <= query_at, s, -1e30)
        top = jnp.max(s, axis=0, keepdims=True)
        p = jnp.exp2(s - top)
        state.append((top, jnp.sum(p, axis=0, keepdims=True), weighted(v[:seen], p.astype(BF16))))

    def step(j, state):
        there = pl.ds(pl.multiple_of(j * rows, rows), rows)
        keys, values = k_scr[there, :], v_scr[there, :]
        blocks = [scores(keys, query) for query in queries]
        out = []
        for s, (top, total, acc) in zip(blocks, state):
            new_top = jnp.maximum(top, jnp.max(s, axis=0, keepdims=True))
            shrink = jnp.exp2(top - new_top)
            p = jnp.exp2(s - new_top)
            total = total * shrink + jnp.sum(p, axis=0, keepdims=True)
            out.append((new_top, total, acc * shrink + weighted(values, p.astype(BF16))))
        return tuple(out)

    state = lax.fori_loop(0, i, step, tuple(state))
    result = jnp.concatenate([acc / total for _, total, acc in state], axis=1)[:head_dim].astype(BF16)
    for n in range(rows // share):
        o_ref[n] = result[:, n * share : (n + 1) * share]


def attention(gathered, w_head, share, head_dim):
    shares, _, width = gathered.shape
    group = math.gcd(4, shares)
    part = 2 * share if group % 2 == 0 else share
    tokens = shares * share
    flops = 2 * tokens * width * 3 * LANES + 4 * tokens * tokens * LANES
    return pl.pallas_call(
        functools.partial(attention_kernel, 1.0 / math.sqrt(head_dim), part, share, head_dim),
        grid=(shares // group,),
        out_shape=jax.ShapeDtypeStruct((shares, head_dim, share), BF16),
        in_specs=[pl.BlockSpec((group, share, width), lambda i: (i, 0, 0)), pl.BlockSpec((width, 3 * LANES), lambda i: (0, 0))],
        out_specs=pl.BlockSpec((group, head_dim, share), lambda i: (i, 0, 0)),
        scratch_shapes=[pltpu.VMEM((tokens, LANES), BF16), pltpu.VMEM((tokens, LANES), BF16)],
        cost_estimate=pl.CostEstimate(flops=flops, bytes_accessed=2 * tokens * width, transcendentals=tokens * tokens // 2),
        compiler_params=pltpu.CompilerParams(dimension_semantics=("arbitrary",), vmem_limit_bytes=60 * 1024 * 1024),
        name="attention",
    )(gathered, w_head)


def mlp_kernel(parts, *refs):
    rows_ref, weights = refs[0], refs[1 : 1 + 3 * parts]
    own_ref, other_ref, up_all, down_all, act_all, turned, sems = refs[1 + 3 * parts :]
    half = own_ref.shape[0]
    units = up_all.shape[0] // parts

    def fetch(m, which):
        to = (up_all, down_all)[which].at[pl.ds(m * units, units)]
        return pltpu.make_async_copy(weights[3 * m + 2 * which], to, sems.at[which, m])

    for which in range(2):
        for m in range(parts):
            fetch(m, which).start()
    turned[...] = rows_ref[...].T
    for m in range(parts):
        fetch(m, 0).wait()
        here = slice(m * units, (m + 1) * units)
        pre_act = jnp.dot(up_all[here, :], turned[...], preferred_element_type=F32) + weights[3 * m + 1][...].T
        act_all[here, :] = jax.nn.gelu(pre_act, approximate=True).astype(BF16)
    for m in range(parts):
        fetch(m, 1).wait()
    for n, out_ref in enumerate((own_ref, other_ref)):
        act = act_all[:, n * half : (n + 1) * half]
        out_ref[...] = lax.dot_general(act, down_all[...], (((0,), (0,)), ((), ())), preferred_element_type=F32)


def mlp(both, weights):
    rows, width = both.shape
    units, parts = weights[0][0].shape[0], len(weights)
    whole, far = pl.BlockSpec(memory_space=pltpu.VMEM), pl.BlockSpec(memory_space=pl.ANY)
    return pl.pallas_call(
        functools.partial(mlp_kernel, parts),
        out_shape=[jax.ShapeDtypeStruct((rows // 2, width), F32)] * 2,
        in_specs=[whole] + [far, whole, far] * parts,
        out_specs=[whole, whole],
        scratch_shapes=[
            pltpu.VMEM((parts * units, width), BF16),
            pltpu.VMEM((parts * units, width), BF16),
            pltpu.VMEM((parts * units, rows), BF16),
            pltpu.VMEM((width, rows), BF16),
            pltpu.SemaphoreType.DMA((2, parts)),
        ],
        cost_estimate=pl.CostEstimate(flops=4 * rows * width * units * parts, bytes_accessed=4 * units * width * parts, transcendentals=rows * units * parts),
        compiler_params=pltpu.CompilerParams(vmem_limit_bytes=60 * 1024 * 1024),
        name="mlp",
    )(both, *[x for up, bias, down in weights for x in (up, bias[None], down)])


def solution(mesh):
    tp_size, dp_size = mesh.shape["tp"], mesh.shape["dp"]
    bits = [1 << n for n in range(dp_size.bit_length() - 1)]

    def spread(block, order):
        held = {0: block}
        for bit in order:
            pairs = [(d, d ^ bit) for d in range(dp_size)]
            held.update({off ^ bit: lax.ppermute(b, "dp", pairs) for off, b in list(held.items())})
        return held

    def partner(x):
        return lax.ppermute(x, "tp", [(t, t ^ 1) for t in range(tp_size)])

    def forward(x_local, ln1_gain, ln1_bias, ln2_gain, ln2_bias, w_qkv, w_out, b_out, w_up, b_up, w_down, b_down):
        layers, width, hidden = w_up.shape
        share, head_dim = x_local.shape[1], w_out.shape[2]
        mine = lax.axis_index("dp")
        core = lax.rem(lax.axis_index("tp"), 2)
        part = hidden // dp_size

        def of_my_core(x):
            x = x.reshape(tp_size // 2, 2, *x.shape[1:])
            return lax.dynamic_index_in_dim(x, core, 1, keepdims=False)

        b_up_all = lax.all_gather(b_up, "tp", axis=0)
        x_local, b_up_all = lax.optimization_barrier((x_local, b_up_all))
        b_up_all = of_my_core(b_up_all).reshape(tp_size // 2, layers, dp_size, part)

        def stacked(layer):
            up = lax.dynamic_slice(w_up, (layer, 0, mine * part), (1, width, part))[0].T
            down = lax.dynamic_slice(w_down, (layer, mine * part, 0), (1, part, width))[0]
            return jnp.concatenate([up, down], 0)

        def mlp_weights(layer, to_pair, after):
            pair = lax.all_gather(to_pair, "tp", axis=0)
            if after is not None:
                pair, _ = lax.optimization_barrier((pair, after))
            pair = pair.reshape(tp_size // 2, 2, 2, part, width)
            up, down = (lax.dynamic_slice(pair, (0, core, n, 0, 0), (tp_size // 2, 1, 1, part, width)).reshape(-1, width) for n in range(2))
            ups, downs = spread(up, bits), spread(down, bits[::-1])
            out = []
            for off in range(dp_size):
                bias = lax.dynamic_index_in_dim(b_up_all[:, layer], mine ^ off, 1, keepdims=False).reshape(-1)
                out.append((ups[off], bias, downs[off]))
            return out

        weights = mlp_weights(0, stacked(0), None)
        resid = x_local[0].astype(F32)
        for layer in range(layers):
            w_head = jnp.pad(w_qkv[layer][:, :, 0], ((0, 0), (0, 0), (0, LANES - head_dim))).reshape(width, 3 * LANES)
            normed = layer_norm(resid, ln1_gain[layer], ln1_bias[layer])
            if layer == 0:
                normed, to_pair = lax.optimization_barrier((normed, stacked(1)))
            to_send = jnp.concatenate([normed, w_out[layer][0]], 0) if layer == 0 else normed
            gathered = lax.all_gather(to_send, "tp", axis=0)
            gathered, _ = lax.optimization_barrier((gathered, [w[::2] for w in weights[:1]]))
            heads = attention(gathered, w_head, share, head_dim)
            heads = lax.all_to_all(heads, "tp", 0, 0, tiled=True).reshape(-1, share)
            if layer == 0:
                w_out_all = gathered[:, share:].reshape(-1, width)
            else:
                w_out_all = lax.all_gather(w_out[layer][0], "tp", axis=0, tiled=True)
            attn = lax.dot_general(heads, w_out_all, (((0,), (0,)), ((), ())), preferred_element_type=F32)
            resid = resid + (attn + b_out[layer])
            normed_mlp = layer_norm(resid, ln2_gain[layer], ln2_bias[layer])
            both = jnp.concatenate([normed_mlp, partner(normed_mlp)], 0)
            ahead = mlp_weights(layer + 1, to_pair, normed_mlp) if layer + 1 < layers else None
            own, other = mlp(both, weights)
            summed = own + partner(other)
            resid = resid + (summed + b_down[layer])
            weights = ahead
        return resid.astype(BF16)[None]

    rows_spec = P("dp", "tp", None)
    in_specs = (rows_spec, P(), P(), P(), P(), P(None, None, None, "tp", None), P(None, "tp", None, None), P(), P(None, None, "tp"), P(None, "tp"), P(None, "tp", None), P())
    return jax.shard_map(forward, mesh=mesh, in_specs=in_specs, out_specs=rows_spec, check_vma=False)
```

profile of v0, /device:TPU:53, one launch (start us, length us, event | category | flops | bytes accessed | tf_op | source)
XLA Modules:
  0.0 562.6 jit_solution(5327000194409045531)
XLA Ops:
  6.6 1.7 constant_dynamic-slice_fusion.13
  8.4 1.1 dynamic-slice_bitcast_fusion
  9.6 0.9 pad_maximum_fusion.4
  10.7 19.8 %all-gather.6 = f32[16,2,384]{2,1,0:T(2,128)S(1)} all-gather(f32[1,2,384]{2,1,0:T(2,128)S(1)} %bitcast.82), channel_id=2, replica_groups=mesh['dp'=4,'tp'=16] {'tp'}, dimensions={0}, use_global_device_ids=true | all-gather | bytes 52224 | tf_op jit(solution)/shard_map/all_gather | solution.py:161
  30.8 0.3 fusion.22
  31.2 0.9 pad_maximum_fusion.3
  32.0 0.4 fusion.25
  32.4 0.7 fusion.36
  33.2 1.1 pad_maximum_fusion.2
  34.4 0.7 all-gather.19.cloned.1.call-update
  35.1 1.0 slice_bitcast_fusion
  36.2 1.4 copy.25.w_ref
  37.7 32.3 %all-gather.15.cloned.1.call-done = bf16[3072,1536]{1,0:T(8,128)(2,1)} async-done(((bf16[192,1536]{1,0:T(8,128)(2,1)}), bf16[3072,1536]{1,0:T(8,128)(2,1)}) %all-gather.15.cloned.1.call-update) | async-done | bytes 9437200 | tf_op jit(solution)/shard_map/all_gather | solution.py:171
  70.0 4.9 constant_dynamic-slice_fusion.11
  74.9 1.2 collective-permute-start.1
  76.1 1.2 collective-permute-start.4
  77.3 87.4 %all-gather.13.cloned.1.call-done = bf16[5632,1536]{1,0:T(8,128)(2,1)} async-done(((bf16[352,1536]{1,0:T(8,128)(2,1)}), bf16[5632,1536]{1,0:T(8,128)(2,1)}) %all-gather.13.cloned.1.call-update) | async-done | bytes 17301520 | tf_op jit(solution)/shard_map/all_gather | solution.py:191
  164.7 24.8 %attention.2 = bf16[16,96,256]{2,1,0:T(8,128)(2,1)} custom-call(bf16[16,352,1536]{2,1,0:T(8,128)(2,1)} %bitcast.83, bf16[1536,384]{1,0:T(8,128)(2,1)} %copy.25.w_ref), custom_call_target="tpu_custom_call" | custom-call | flops 13421772800 | bytes 12582912 | tf_op jit(solution)/shard_map/attention/pallas_call | solution.py:75
  189.5 6.6 %all-to-all-start = ((bf16[16,96,256]{2,1,0:T(8,128)(2,1)}), bf16[16,96,256]{2,1,0:T(8,128)(2,1)S(1)}, u32[]{:S(2)}, u32[]{:S(2)}) async-start(bf16[16,96,256]{2,1,0:T(8,128)(2,1)} %attention.2), calls=%async_computation | async-start | bytes 1572864 | tf_op jit(solution)/shard_map/all_to_all | solution.py:194
  196.3 1.3 collective-permute-start.2
  197.6 1.2 collective-permute-start.3
  199.4 23.8 %all-to-all-done = bf16[16,96,256]{2,1,0:T(8,128)(2,1)S(1)} async-done(((bf16[16,96,256]{2,1,0:T(8,128)(2,1)}), bf16[16,96,256]{2,1,0:T(8,128)(2,1)S(1)}, u32[]{:S(2)}, u32[]{:S(2)}) %all-to-all-start) | async-done | bytes 786464 | tf_op jit(solution)/shard_map/all_to_all | solution.py:194
  223.1 3.9 fusion.38
  227.7 0.6 collective-permute-start
  228.6 0.7 broadcast_in_dim_reshape.24.refs_2_
  229.3 0.7 broadcast_in_dim_reshape.25.refs_5_
  229.9 0.7 broadcast_in_dim_reshape.26.refs_8_
  230.6 0.7 broadcast_in_dim_reshape.27.refs_11_
  231.3 1.3 pad_maximum_fusion.refs_0_
  232.5 16.6 %collective-permute-done.2.refs_6_ = bf16[768,1536]{1,0:T(8,128)(2,1)} collective-permute-done((bf16[768,1536]{1,0:T(8,128)(2,1)}, bf16[768,1536]{1,0:T(8,128)(2,1)}, u32[]{:S(2)}, u32[]{:S(2)}) %collective-permute-start.2) | collective-permute-done | bytes 2359328 | tf_op jit(solution)/shard_map/ppermute | solution.py:144
  249.2 0.9 collective-permute-done.3.refs_7_
  250.1 50.6 %collective-permute-done.5.refs_10_ = bf16[768,1536]{1,0:T(8,128)(2,1)} collective-permute-done((bf16[768,1536]{1,0:T(8,128)(2,1)}, bf16[768,1536]{1,0:T(8,128)(2,1)}, u32[]{:S(2)}, u32[]{:S(2)}) %collective-permute-start.5) | collective-permute-done | bytes 2359328 | tf_op jit(solution)/shard_map/ppermute | solution.py:144
  300.6 16.4 %mlp.2 = (f32[256,1536]{1,0:T(8,128)}, f32[256,1536]{1,0:T(8,128)}) custom-call(bf16[512,1536]{1,0:T(8,128)(2,1)} %pad_maximum_fusion.refs_0_, bf16[768,1536]{1,0:T(8,128)(2,1)} %bitcast.11.refs_1_, f32[1,768]{1,0:T(1,128)} %broadcast_in_dim_reshape.24.refs_2_, bf16[768,1536]{1,0:T(8,128)(2,1)} %bitcast.12.refs_3_, ...), custom_call_target="tpu_custom_call" | custom-call | flops 9663676416 | bytes 18874368 | tf_op jit(solution)/shard_map/mlp/pallas_call | solution.py:118
  317.0 1.6 collective-permute-start.7
  318.7 3.2 collective-permute-done.7
  321.9 1.8 fusion.35
  324.1 1.2 add_convert_fusion.2
  325.4 0.6 all-gather.21.cloned.1.call-update
  326.0 1.3 pad.8
  327.3 1.4 copy.28.w_ref
  328.7 5.0 constant_dynamic-slice_fusion.4
  334.0 1.4 collective-permute-start.12
  335.4 60.9 %all-gather.17.cloned.1.call-done = bf16[4096,1536]{1,0:T(8,128)(2,1)} async-done(((bf16[256,1536]{1,0:T(8,128)(2,1)}), bf16[4096,1536]{1,0:T(8,128)(2,1)}) %all-gather.17.cloned.1.call-update) | async-done | bytes 12582928 | tf_op jit(solution)/shard_map/all_gather | solution.py:191
  396.3 24.7 %attention.3 = bf16[16,96,256]{2,1,0:T(8,128)(2,1)} custom-call(bf16[16,256,1536]{2,1,0:T(8,128)(2,1)} %bitcast.85, bf16[1536,384]{1,0:T(8,128)(2,1)} %copy.28.w_ref), custom_call_target="tpu_custom_call" | custom-call | flops 13421772800 | bytes 12582912 | tf_op jit(solution)/shard_map/attention/pallas_call | solution.py:75
  421.0 6.4 %all-to-all-start.1 = ((bf16[16,96,256]{2,1,0:T(8,128)(2,1)}), bf16[16,96,256]{2,1,0:T(8,128)(2,1)S(1)}, u32[]{:S(2)}, u32[]{:S(2)}) async-start(bf16[16,96,256]{2,1,0:T(8,128)(2,1)} %attention.3), calls=%async_computation.1 | async-start | bytes 1572864 | tf_op jit(solution)/shard_map/all_to_all | solution.py:194
  427.4 1.2 collective-permute-start.10
  428.7 1.2 collective-permute-start.11
  430.4 16.9 %all-gather.21.cloned.1.call-done = bf16[1,1,1536,1536]{3,2,1,0:T(8,128)(2,1)} async-done(((bf16[1,1,96,1536]{3,2,1,0:T(8,128)(2,1)}), bf16[1,1,1536,1536]{3,2,1,0:T(8,128)(2,1)}) %all-gather.21.cloned.1.call-update) | async-done | bytes 4718608 | tf_op jit(solution)/shard_map/all_gather | solution.py:198
  447.3 2.5 all-to-all-done.1
  449.8 0.9 copy-done.2
  450.7 4.1 fusion.39
  455.4 0.5 collective-permute-start.8
  455.9 0.7 broadcast_in_dim_reshape.28.refs_2_
  456.6 0.7 broadcast_in_dim_reshape.29.refs_5_
  457.3 0.7 broadcast_in_dim_reshape.30.refs_8_
  457.9 0.7 broadcast_in_dim_reshape.31.refs_11_
  458.6 1.3 pad_maximum_fusion.1.refs_0_
  459.9 20.3 %collective-permute-done.10.refs_6_ = bf16[768,1536]{1,0:T(8,128)(2,1)} collective-permute-done((bf16[768,1536]{1,0:T(8,128)(2,1)}, bf16[768,1536]{1,0:T(8,128)(2,1)}, u32[]{:S(2)}, u32[]{:S(2)}) %collective-permute-start.10) | collective-permute-done | bytes 2359328 | tf_op jit(solution)/shard_map/ppermute | solution.py:144
  480.2 0.9 collective-permute-done.11.refs_7_
  481.1 50.6 %collective-permute-done.13.refs_10_ = bf16[768,1536]{1,0:T(8,128)(2,1)} collective-permute-done((bf16[768,1536]{1,0:T(8,128)(2,1)}, bf16[768,1536]{1,0:T(8,128)(2,1)}, u32[]{:S(2)}, u32[]{:S(2)}) %collective-permute-start.13) | collective-permute-done | bytes 2359328 | tf_op jit(solution)/shard_map/ppermute | solution.py:144
  531.7 16.5 %mlp.3 = (f32[256,1536]{1,0:T(8,128)}, f32[256,1536]{1,0:T(8,128)}) custom-call(bf16[512,1536]{1,0:T(8,128)(2,1)} %pad_maximum_fusion.1.refs_0_, bf16[768,1536]{1,0:T(8,128)(2,1)} %bitcast.21.refs_1_, f32[1,768]{1,0:T(1,128)} %broadcast_in_dim_reshape.28.refs_2_, bf16[768,1536]{1,0:T(8,128)(2,1)} %bitcast.22.refs_3_, ...), custom_call_target="tpu_custom_call" | custom-call | flops 9663676416 | bytes 18874368 | tf_op jit(solution)/shard_map/mlp/pallas_call | solution.py:118
  548.1 1.6 collective-permute-start.15
  549.8 3.2 collective-permute-done.15
  553.0 2.8 fusion.26
  (69 shorter events, 4.5 us)
Async XLA Ops:
  6.5 63.4 %all-gather.15.cloned.1.call-start = ((), (), s32[]{:S(2)}) async-start(), calls=%async_computation.3 | async-start | bytes 10027008 | tf_op jit(solution)/shard_map/all_gather | solution.py:171
  8.4 2.3 copy-start.10
  8.4 22.1 %copy-start.4 = (f32[2,1536]{1,0:T(2,128)S(1)}, f32[2,1536]{1,0:T(2,128)}, u32[]{:S(2)}) copy-start(f32[2,1536]{1,0:T(2,128)} %param.14) | copy-start | bytes 36868
  8.4 22.1 %copy-start.5 = (f32[2,1536]{1,0:T(2,128)S(1)}, f32[2,1536]{1,0:T(2,128)}, u32[]{:S(2)}) copy-start(f32[2,1536]{1,0:T(2,128)} %param.13) | copy-start | bytes 36868
  9.5 21.0 %copy-start = (bf16[1,256,1536]{2,1,0:T(8,128)(2,1)S(1)}, bf16[1,256,1536]{2,1,0:T(8,128)(2,1)}, u32[]{:S(2)}) copy-start(bf16[1,256,1536]{2,1,0:T(8,128)(2,1)} %param.12) | copy-start | bytes 2359300
  10.5 154.3 %all-gather.13.cloned.1.call-start = ((), (), s32[]{:S(2)}) async-start(), calls=%async_computation.2 | async-start | bytes 18382848 | tf_op jit(solution)/shard_map/all_gather | solution.py:191
  31.1 1.3 copy-start.3
  33.2 1.9 copy-start.1
  34.3 294.4 %all-gather.19.cloned.1.call-start = ((), (), s32[]{:S(2)}) async-start(), calls=%async_computation.5 | async-start | bytes 10027008 | tf_op jit(solution)/shard_map/all_gather | solution.py:171
  74.9 123.9 %collective-permute-start.1 = (bf16[768,1536]{1,0:T(8,128)(2,1)}, bf16[768,1536]{1,0:T(8,128)(2,1)}, u32[]{:S(2)}, u32[]{:S(2)}) collective-permute-start(bf16[768,1536]{1,0:T(8,128)(2,1)} %bitcast.11.refs_1_), channel_id=1, source_target_pairs={{0,16},{16,0},{32,48},{48,32},{1,17},{17,1},{33,49},{49,33},{2,18}... | collective-permute-start | bytes 7077896 | tf_op jit(solution)/shard_map/ppermute | solution.py:144
  76.1 123.0 %collective-permute-start.4 = (bf16[768,1536]{1,0:T(8,128)(2,1)}, bf16[768,1536]{1,0:T(8,128)(2,1)}, u32[]{:S(2)}, u32[]{:S(2)}) collective-permute-start(bf16[768,1536]{1,0:T(8,128)(2,1)} %bitcast.12.refs_3_), channel_id=1, source_target_pairs={{0,32},{16,48},{32,0},{48,16},{1,33},{17,49},{33,1},{49,17},{2,34}... | collective-permute-start | bytes 7077896 | tf_op jit(solution)/shard_map/ppermute | solution.py:144
  189.5 6.7 %copy-start.6 = (f32[2,1536]{1,0:T(2,128)S(1)}, f32[2,1536]{1,0:T(2,128)}, u32[]{:S(2)}) copy-start(f32[2,1536]{1,0:T(2,128)} %param.19) | copy-start | bytes 36868
  189.5 6.7 %copy-start.7 = (f32[2,1536]{1,0:T(2,128)S(1)}, f32[2,1536]{1,0:T(2,128)}, u32[]{:S(2)}) copy-start(f32[2,1536]{1,0:T(2,128)} %param.16) | copy-start | bytes 36868
  189.5 6.7 %copy-start.8 = (f32[2,1536]{1,0:T(2,128)S(1)}, f32[2,1536]{1,0:T(2,128)}, u32[]{:S(2)}) copy-start(f32[2,1536]{1,0:T(2,128)} %param.15) | copy-start | bytes 36868
  189.5 33.6 %all-to-all-start = ((bf16[16,96,256]{2,1,0:T(8,128)(2,1)}), bf16[16,96,256]{2,1,0:T(8,128)(2,1)S(1)}, u32[]{:S(2)}, u32[]{:S(2)}) async-start(bf16[16,96,256]{2,1,0:T(8,128)(2,1)} %attention.2), calls=%async_computation | async-start | bytes 1572864 | tf_op jit(solution)/shard_map/all_to_all | solution.py:194
  196.1 200.2 %all-gather.17.cloned.1.call-start = ((), (), s32[]{:S(2)}) async-start(), calls=%async_computation.4 | async-start | bytes 13369344 | tf_op jit(solution)/shard_map/all_gather | solution.py:191
  196.3 52.8 %collective-permute-start.2 = (bf16[768,1536]{1,0:T(8,128)(2,1)}, bf16[768,1536]{1,0:T(8,128)(2,1)}, u32[]{:S(2)}, u32[]{:S(2)}) collective-permute-start(bf16[768,1536]{1,0:T(8,128)(2,1)} %bitcast.12.refs_3_), channel_id=1, source_target_pairs={{0,16},{16,0},{32,48},{48,32},{1,17},{17,1},{33,49},{49,33},{2,18}... | collective-permute-start | bytes 7077896 | tf_op jit(solution)/shard_map/ppermute | solution.py:144
  197.6 52.4 %collective-permute-start.3 = (bf16[768,1536]{1,0:T(8,128)(2,1)}, bf16[768,1536]{1,0:T(8,128)(2,1)}, u32[]{:S(2)}, u32[]{:S(2)}) collective-permute-start(bf16[768,1536]{1,0:T(8,128)(2,1)} %bitcast.11.refs_1_), channel_id=1, source_target_pairs={{0,32},{16,48},{32,0},{48,16},{1,33},{17,49},{33,1},{49,17},{2,34}... | collective-permute-start | bytes 7077896 | tf_op jit(solution)/shard_map/ppermute | solution.py:144
  198.8 101.8 %collective-permute-start.5 = (bf16[768,1536]{1,0:T(8,128)(2,1)}, bf16[768,1536]{1,0:T(8,128)(2,1)}, u32[]{:S(2)}, u32[]{:S(2)}) collective-permute-start(bf16[768,1536]{1,0:T(8,128)(2,1)} %collective-permute-done.1.refs_4_), channel_id=1, source_target_pairs={{0,32},{16,48},{32,0},{48,16},{1,33},{17,49},{33,1},{49,17},{2,34}... | collective-permute-start | bytes 7077896 | tf_op jit(solution)/shard_map/ppermute | solution.py:144
  199.1 101.5 %collective-permute-start.6 = (bf16[768,1536]{1,0:T(8,128)(2,1)}, bf16[768,1536]{1,0:T(8,128)(2,1)}, u32[]{:S(2)}, u32[]{:S(2)}) collective-permute-start(bf16[768,1536]{1,0:T(8,128)(2,1)} %collective-permute-done.4.refs_9_), channel_id=1, source_target_pairs={{0,16},{16,0},{32,48},{48,32},{1,17},{17,1},{33,49},{49,33},{2,18}... | collective-permute-start | bytes 7077896 | tf_op jit(solution)/shard_map/ppermute | solution.py:144
  227.7 3.5 collective-permute-start
  232.5 86.1 %copy-start.9 = (f32[2,1536]{1,0:T(2,128)S(1)}, f32[2,1536]{1,0:T(2,128)}, u32[]{:S(2)}) copy-start(f32[2,1536]{1,0:T(2,128)} %param.23) | copy-start | bytes 36868
  317.0 4.9 collective-permute-start.7
  325.4 121.9 %all-gather.21.cloned.1.call-start = ((), (), s32[]{:S(2)}) async-start(), calls=%async_computation.6 | async-start | bytes 5013504 | tf_op jit(solution)/shard_map/all_gather | solution.py:198
  333.7 96.1 %collective-permute-start.9 = (bf16[768,1536]{1,0:T(8,128)(2,1)}, bf16[768,1536]{1,0:T(8,128)(2,1)}, u32[]{:S(2)}, u32[]{:S(2)}) collective-permute-start(bf16[768,1536]{1,0:T(8,128)(2,1)} %bitcast.21.refs_1_), channel_id=1, source_target_pairs={{0,16},{16,0},{32,48},{48,32},{1,17},{17,1},{33,49},{49,33},{2,18}... | collective-permute-start | bytes 7077896 | tf_op jit(solution)/shard_map/ppermute | solution.py:144
  334.0 96.1 %collective-permute-start.12 = (bf16[768,1536]{1,0:T(8,128)(2,1)}, bf16[768,1536]{1,0:T(8,128)(2,1)}, u32[]{:S(2)}, u32[]{:S(2)}) collective-permute-start(bf16[768,1536]{1,0:T(8,128)(2,1)} %bitcast.22.refs_3_), channel_id=1, source_target_pairs={{0,32},{16,48},{32,0},{48,16},{1,33},{17,49},{33,1},{49,17},{2,34}... | collective-permute-start | bytes 7077896 | tf_op jit(solution)/shard_map/ppermute | solution.py:144
  421.0 28.8 %all-to-all-start.1 = ((bf16[16,96,256]{2,1,0:T(8,128)(2,1)}), bf16[16,96,256]{2,1,0:T(8,128)(2,1)S(1)}, u32[]{:S(2)}, u32[]{:S(2)}) async-start(bf16[16,96,256]{2,1,0:T(8,128)(2,1)} %attention.3), calls=%async_computation.1 | async-start | bytes 1572864 | tf_op jit(solution)/shard_map/all_to_all | solution.py:194
  427.4 52.7 %collective-permute-start.10 = (bf16[768,1536]{1,0:T(8,128)(2,1)}, bf16[768,1536]{1,0:T(8,128)(2,1)}, u32[]{:S(2)}, u32[]{:S(2)}) collective-permute-start(bf16[768,1536]{1,0:T(8,128)(2,1)} %bitcast.22.refs_3_), channel_id=1, source_target_pairs={{0,16},{16,0},{32,48},{48,32},{1,17},{17,1},{33,49},{49,33},{2,18}... | collective-permute-start | bytes 7077896 | tf_op jit(solution)/shard_map/ppermute | solution.py:144
  428.7 52.4 %collective-permute-start.11 = (bf16[768,1536]{1,0:T(8,128)(2,1)}, bf16[768,1536]{1,0:T(8,128)(2,1)}, u32[]{:S(2)}, u32[]{:S(2)}) collective-permute-start(bf16[768,1536]{1,0:T(8,128)(2,1)} %bitcast.21.refs_1_), channel_id=1, source_target_pairs={{0,32},{16,48},{32,0},{48,16},{1,33},{17,49},{33,1},{49,17},{2,34}... | collective-permute-start | bytes 7077896 | tf_op jit(solution)/shard_map/ppermute | solution.py:144
  429.8 101.8 %collective-permute-start.13 = (bf16[768,1536]{1,0:T(8,128)(2,1)}, bf16[768,1536]{1,0:T(8,128)(2,1)}, u32[]{:S(2)}, u32[]{:S(2)}) collective-permute-start(bf16[768,1536]{1,0:T(8,128)(2,1)} %collective-permute-done.9.refs_4_), channel_id=1, source_target_pairs={{0,32},{16,48},{32,0},{48,16},{1,33},{17,49},{33,1},{49,17},{2,34}... | collective-permute-start | bytes 7077896 | tf_op jit(solution)/shard_map/ppermute | solution.py:144
  430.1 101.5 %collective-permute-start.14 = (bf16[768,1536]{1,0:T(8,128)(2,1)}, bf16[768,1536]{1,0:T(8,128)(2,1)}, u32[]{:S(2)}, u32[]{:S(2)}) collective-permute-start(bf16[768,1536]{1,0:T(8,128)(2,1)} %collective-permute-done.12.refs_9_), channel_id=1, source_target_pairs={{0,16},{16,0},{32,48},{48,32},{1,17},{17,1},{33,49},{49,33},{2,18}... | collective-permute-start | bytes 7077896 | tf_op jit(solution)/shard_map/ppermute | solution.py:144
  449.8 0.9 copy-start.2
  455.4 3.2 collective-permute-start.8
  548.1 4.9 collective-permute-start.15
Sparse Core Ops, SparseCore 0:
  10.6 59.3 all-gather.14
  71.6 93.0 all-gather.12
  166.4 73.0 all-gather.18
  325.5 70.7 all-gather.16
  397.8 49.4 all-gather.20
where the time goes:
time: 572 us; the launch traced here: 563 us
  waiting for transfers between devices  372 us (65%)
  Pallas kernels  82.4 us (14%)
  starting transfers between devices  27.6 us (5%)
  local copies, waits for them, and re-layouts  25.7 us (4%)
  blocking collectives  19.8 us (3%)
  other arithmetic  13.7 us (2%)
  between operations  13.7 us (2%)
  matrix products  7.99 us (1%)
    all_gather x2, waiting for transfers between devices, forward(): gathered = lax.all_gather(to_send, 'tp', axis=0)  148 us
    ppermute x12, waiting for transfers between devices, spread(): lax.ppermute(b, 'dp', pairs)  140 us
    pallas_call x2, Pallas kernels, attention(): pl.pallas_call(functools.partial(attention_kernel, 1.0 / math.sqrt(head_d...  49.5 us
    pallas_call x2, Pallas kernels, mlp(): pl.pallas_call(functools.partial(mlp_kernel, parts), out_shape=[jax.Shape...  32.9 us
    all_gather x2, waiting for transfers between devices, mlp_weights(): pair = lax.all_gather(to_pair, 'tp', axis=0)  32.3 us
    all_to_all x2, waiting for transfers between devices, forward(): heads = lax.all_to_all(heads, 'tp', 0, 0, tiled=True).reshape(-1, share)  26.3 us
    all_gather x1, blocking collectives, forward(): b_up_all = lax.all_gather(b_up, 'tp', axis=0)  19.8 us
    all_gather x1, waiting for transfers between devices, forward(): w_out_all = lax.all_gather(w_out[layer][0], 'tp', axis=0, tiled=True)  16.9 us
  transfers between devices with their start and end apart: 23, of which 14 were waited for; matrix products, arithmetic and copies ran while one was open for 7% of the time, Pallas kernels for 12%

commit v1 on v0

--- a/solution.py
+++ b/solution.py
@@ -23,18 +23,19 @@
     rows = k_scr.shape[0] // pl.num_programs(0)
     here = pl.ds(pl.multiple_of(i * rows, rows), rows)
     hidden = h_ref[...].reshape(rows, h_ref.shape[-1])
-    qkv = jnp.dot(hidden, w_ref[...], preferred_element_type=F32).astype(BF16)
-    q, k, v = (qkv[:, n * LANES : (n + 1) * LANES] for n in range(3))
+    qkv = lax.dot_general(w_ref[...], hidden, (((1,), (1,)), ((), ())), preferred_element_type=F32).astype(BF16)
+    q, k, v = (qkv[n * head_dim : (n + 1) * head_dim] for n in range(3))
+    k = k.T
     k_scr[here, :] = k
-    v_scr[here, :] = v
+    v_scr[:, here] = v
     to_exp2 = scale * math.log2(math.e)
-    queries = [q[n * part : (n + 1) * part] for n in range(rows // part)]
+    queries = [q[:, n * part : (n + 1) * part] for n in range(rows // part)]
 
     def scores(keys, query):
-        return lax.dot_general(keys, query, (((1,), (1,)), ((), ())), preferred_element_type=F32) * to_exp2
+        return jnp.dot(keys, query, preferred_element_type=F32) * to_exp2
 
     def weighted(values, probs):
-        return lax.dot_general(values, probs, (((0,), (0,)), ((), ())), preferred_element_type=F32)
+        return jnp.dot(values, probs.astype(BF16), preferred_element_type=F32)
 
     state = []
     for n, query in enumerate(queries):
@@ -42,14 +43,14 @@
         s = scores(k[:seen], query)
         key_at = lax.broadcasted_iota(jnp.int32, s.shape, 0)
         query_at = lax.broadcasted_iota(jnp.int32, s.shape, 1) + n * part
-        s = jnp.where(key_at <= query_at, s, -1e30)
+        s = jnp.where(key_at <= query_at, s, -jnp.inf)
         top = jnp.max(s, axis=0, keepdims=True)
         p = jnp.exp2(s - top)
-        state.append((top, jnp.sum(p, axis=0, keepdims=True), weighted(v[:seen], p.astype(BF16))))
+        state.append((top, jnp.sum(p, axis=0, keepdims=True), weighted(v[:, :seen], p)))
 
     def step(j, state):
         there = pl.ds(pl.multiple_of(j * rows, rows), rows)
-        keys, values = k_scr[there, :], v_scr[there, :]
+        keys, values = k_scr[there, :], v_scr[:, there]
         blocks = [scores(keys, query) for query in queries]
         out = []
         for s, (top, total, acc) in zip(blocks, state):
@@ -57,11 +58,11 @@
             shrink = jnp.exp2(top - new_top)
             p = jnp.exp2(s - new_top)
             total = total * shrink + jnp.sum(p, axis=0, keepdims=True)
-            out.append((new_top, total, acc * shrink + weighted(values, p.astype(BF16))))
+            out.append((new_top, total, acc * shrink + weighted(values, p)))
         return tuple(out)
 
     state = lax.fori_loop(0, i, step, tuple(state))
-    result = jnp.concatenate([acc / total for _, total, acc in state], axis=1)[:head_dim].astype(BF16)
+    result = jnp.concatenate([acc / total for _, total, acc in state], axis=1).astype(BF16)
     for n in range(rows // share):
         o_ref[n] = result[:, n * share : (n + 1) * share]
 
@@ -71,54 +72,68 @@
     group = math.gcd(4, shares)
     part = 2 * share if group % 2 == 0 else share
     tokens = shares * share
-    flops = 2 * tokens * width * 3 * LANES + 4 * tokens * tokens * LANES
+    flops = 6 * tokens * width * head_dim + 4 * tokens * tokens * head_dim
     return pl.pallas_call(
         functools.partial(attention_kernel, 1.0 / math.sqrt(head_dim), part, share, head_dim),
         grid=(shares // group,),
         out_shape=jax.ShapeDtypeStruct((shares, head_dim, share), BF16),
-        in_specs=[pl.BlockSpec((group, share, width), lambda i: (i, 0, 0)), pl.BlockSpec((width, 3 * LANES), lambda i: (0, 0))],
+        in_specs=[pl.BlockSpec((group, share, width), lambda i: (i, 0, 0)), pl.BlockSpec((3 * head_dim, width), lambda i: (0, 0))],
         out_specs=pl.BlockSpec((group, head_dim, share), lambda i: (i, 0, 0)),
-        scratch_shapes=[pltpu.VMEM((tokens, LANES), BF16), pltpu.VMEM((tokens, LANES), BF16)],
+        scratch_shapes=[pltpu.VMEM((tokens, head_dim), BF16), pltpu.VMEM((head_dim, tokens), BF16)],
         cost_estimate=pl.CostEstimate(flops=flops, bytes_accessed=2 * tokens * width, transcendentals=tokens * tokens // 2),
         compiler_params=pltpu.CompilerParams(dimension_semantics=("arbitrary",), vmem_limit_bytes=60 * 1024 * 1024),
         name="attention",
     )(gathered, w_head)
 
 
-def mlp_kernel(parts, *refs):
-    rows_ref, weights = refs[0], refs[1 : 1 + 3 * parts]
-    own_ref, other_ref, up_all, down_all, act_all, turned, sems = refs[1 + 3 * parts :]
-    half = own_ref.shape[0]
+def mlp_kernel(parts, rows_ref, bias_ref, *refs):
+    weights = refs[: 2 * parts]
+    own_ref, other_ref, up_all, down_all, act_all, turned, sems = refs[2 * parts :]
+    half, width = own_ref.shape
     units = up_all.shape[0] // parts
 
-    def fetch(m, which):
-        to = (up_all, down_all)[which].at[pl.ds(m * units, units)]
-        return pltpu.make_async_copy(weights[3 * m + 2 * which], to, sems.at[which, m])
+    def part_of(m):
+        return pl.ds(pl.multiple_of(m * units, 16), units)
+
+    def fetch(m, which, source):
+        return pltpu.make_async_copy(weights[2 * source + which], (up_all, down_all)[which].at[part_of(m)], sems.at[which, m])
 
     for which in range(2):
         for m in range(parts):
-            fetch(m, which).start()
+            fetch(m, which, m).start()
     turned[...] = rows_ref[...].T
+
+    def lift(m, carry):
+        fetch(m, 0, 0).wait()
+        here = part_of(m)
+        pre_act = jnp.dot(up_all[here, :], turned[...], preferred_element_type=F32) + bias_ref[m].T
+        act_all[here, :] = jax.nn.gelu(pre_act, approximate=True).astype(BF16)
+        return carry
+
+    lax.fori_loop(0, parts, lift, 0)
     for m in range(parts):
-        fetch(m, 0).wait()
-        here = slice(m * units, (m + 1) * units)
-        pre_act = jnp.dot(up_all[here, :], turned[...], preferred_element_type=F32) + weights[3 * m + 1][...].T
-        act_all[here, :] = jax.nn.gelu(pre_act, approximate=True).astype(BF16)
-    for m in range(parts):
-        fetch(m, 1).wait()
-    for n, out_ref in enumerate((own_ref, other_ref)):
-        act = act_all[:, n * half : (n + 1) * half]
-        out_ref[...] = lax.dot_general(act, down_all[...], (((0,), (0,)), ((), ())), preferred_element_type=F32)
+        fetch(m, 1, m).wait()
+    tile = math.gcd(width, 4 * LANES)
+
+    def lower(n, carry):
+        columns = pl.ds(pl.multiple_of(n * tile, tile), tile)
+        result = lax.dot_general(act_all[...], down_all[:, columns], (((0,), (0,)), ((), ())), preferred_element_type=F32)
+        own_ref[:, columns] = result[:half]
+        other_ref[:, columns] = result[half:]
+        return carry
+
+    lax.fori_loop(0, width // tile, lower, 0)
 
 
 def mlp(both, weights):
     rows, width = both.shape
     units, parts = weights[0][0].shape[0], len(weights)
     whole, far = pl.BlockSpec(memory_space=pltpu.VMEM), pl.BlockSpec(memory_space=pl.ANY)
+    bias = jnp.stack([bias[None] for _, bias, _ in weights])
     return pl.pallas_call(
         functools.partial(mlp_kernel, parts),
         out_shape=[jax.ShapeDtypeStruct((rows // 2, width), F32)] * 2,
-        in_specs=[whole] + [far, whole, far] * parts,
+        in_specs=[whole] * 2 + [far] * (2 * parts),
         out_specs=[whole, whole],
         scratch_shapes=[
             pltpu.VMEM((parts * units, width), BF16),
@@ -130,7 +145,7 @@
         cost_estimate=pl.CostEstimate(flops=4 * rows * width * units * parts, bytes_accessed=4 * units * width * parts, transcendentals=rows * units * parts),
         compiler_params=pltpu.CompilerParams(vmem_limit_bytes=60 * 1024 * 1024),
         name="mlp",
-    )(both, *[x for up, bias, down in weights for x in (up, bias[None], down)])
+    )(both, bias, *[x for up, _, down in weights for x in (up, down)])
 
 
 def solution(mesh):
@@ -183,7 +198,7 @@
         weights = mlp_weights(0, stacked(0), None)
         resid = x_local[0].astype(F32)
         for layer in range(layers):
-            w_head = jnp.pad(w_qkv[layer][:, :, 0], ((0, 0), (0, 0), (0, LANES - head_dim))).reshape(width, 3 * LANES)
+            w_head = w_qkv[layer][:, :, 0].reshape(width, 3 * head_dim).T
             normed = layer_norm(resid, ln1_gain[layer], ln1_bias[layer])
             if layer == 0:
                 normed, to_pair = lax.optimization_barrier((normed, stacked(1)))

time: 572 us -> 559 us (0.977); the launches traced: 563 us -> 557 us
  local copies, waits for them, and re-layouts: 25.7 us -> 17.2 us
  waiting for transfers between devices: 372 us -> 379 us
    all_gather x1, waiting for transfers between devices: 16.9 us -> 24.1 us  [forward(): w_out_all = lax.all_gather(w_out[layer][0], 'tp', axis=0, tiled=True)]
    pallas_call x2, Pallas kernels: 49.5 us -> 42.8 us  [attention(): pl.pallas_call(functools.partial(attention_kernel, 1.0 / math.sqrt(head_d...]
  transfers between devices with their start and end apart: 23 -> 23, of which waited for: 14 -> 15; matrix products, arithmetic and copies ran while one was open for 7% -> 6% of each run, Pallas kernels for 12% -> 11%
where the time goes in v1:
time: 559 us; the launch traced here: 557 us
  waiting for transfers between devices  379 us (68%)
  Pallas kernels  77 us (14%)
  starting transfers between devices  27.3 us (5%)
  blocking collectives  19.8 us (4%)
  local copies, waits for them, and re-layouts  17.2 us (3%)
  other arithmetic  14.9 us (3%)
  between operations  13.5 us (2%)
  matrix products  7.99 us (1%)
    all_gather x2, waiting for transfers between devices, forward(): gathered = lax.all_gather(to_send, 'tp', axis=0)  151 us
    ppermute x12, waiting for transfers between devices, spread(): lax.ppermute(b, 'dp', pairs)  137 us
    pallas_call x2, Pallas kernels, attention(): pl.pallas_call(functools.partial(attention_kernel, 1.0 / math.sqrt(head_d...  42.8 us
    pallas_call x2, Pallas kernels, mlp(): pl.pallas_call(functools.partial(mlp_kernel, parts), out_shape=[jax.Shape...  34.2 us
    all_gather x2, waiting for transfers between devices, mlp_weights(): pair = lax.all_gather(to_pair, 'tp', axis=0)  33.6 us
    all_gather x1, waiting for transfers between devices, forward(): w_out_all = lax.all_gather(w_out[layer][0], 'tp', axis=0, tiled=True)  24.1 us
    all_to_all x2, waiting for transfers between devices, forward(): heads = lax.all_to_all(heads, 'tp', 0, 0, tiled=True).reshape(-1, share)  23.8 us
    all_gather x1, blocking collectives, forward(): b_up_all = lax.all_gather(b_up, 'tp', axis=0)  19.8 us
  transfers between devices with their start and end apart: 23, of which 15 were waited for; matrix products, arithmetic and copies ran while one was open for 6% of the time, Pallas kernels for 11%

profile of v1, /device:TPU:53, one launch (start us, length us, event | category | flops | bytes accessed | tf_op | source)
XLA Modules:
  0.0 557.0 jit_solution(1249467649930458592)
XLA Ops:
  6.6 1.7 constant_dynamic-slice_fusion.13
  8.4 1.1 dynamic-slice_bitcast_fusion
  9.6 0.9 pad_maximum_fusion.4
  10.7 19.8 %all-gather.6 = f32[16,2,384]{2,1,0:T(2,128)S(1)} all-gather(f32[1,2,384]{2,1,0:T(2,128)S(1)} %bitcast.79), channel_id=2, replica_groups=mesh['dp'=4,'tp'=16] {'tp'}, dimensions={0}, use_global_device_ids=true | all-gather | bytes 52224 | tf_op jit(solution)/shard_map/all_gather | solution.py:176
  30.8 0.3 fusion.22
  31.2 0.9 pad_maximum_fusion.3
  32.0 0.4 fusion.25
  32.4 0.7 fusion.37
  33.2 1.1 pad_maximum_fusion.2
  34.4 0.7 all-gather.19.cloned.1.call-update
  35.1 1.3 fusion.36
  36.4 33.5 %all-gather.15.cloned.1.call-done = bf16[3072,1536]{1,0:T(8,128)(2,1)} async-done(((bf16[192,1536]{1,0:T(8,128)(2,1)}), bf16[3072,1536]{1,0:T(8,128)(2,1)}) %all-gather.15.cloned.1.call-update) | async-done | bytes 9437200 | tf_op jit(solution)/shard_map/all_gather | solution.py:186
  70.0 4.9 constant_dynamic-slice_fusion.11
  74.9 1.2 collective-permute-start.1
  76.1 1.2 collective-permute-start.4
  77.3 87.4 %all-gather.13.cloned.1.call-done = bf16[5632,1536]{1,0:T(8,128)(2,1)} async-done(((bf16[352,1536]{1,0:T(8,128)(2,1)}), bf16[5632,1536]{1,0:T(8,128)(2,1)}) %all-gather.13.cloned.1.call-update) | async-done | bytes 17301520 | tf_op jit(solution)/shard_map/all_gather | solution.py:206
  164.7 21.4 %attention.2 = bf16[16,96,256]{2,1,0:T(8,128)(2,1)} custom-call(bf16[16,352,1536]{2,1,0:T(8,128)(2,1)} %bitcast.80, bf16[288,1536]{1,0:T(8,128)(2,1)} %bitcast.76), custom_call_target="tpu_custom_call" | custom-call | flops 10066329600 | bytes 12582912 | tf_op jit(solution)/shard_map/attention/pallas_call | solution.py:76
  186.2 6.6 %all-to-all-start = ((bf16[16,96,256]{2,1,0:T(8,128)(2,1)}), bf16[16,96,256]{2,1,0:T(8,128)(2,1)S(1)}, u32[]{:S(2)}, u32[]{:S(2)}) async-start(bf16[16,96,256]{2,1,0:T(8,128)(2,1)} %attention.2), calls=%async_computation | async-start | bytes 1572864 | tf_op jit(solution)/shard_map/all_to_all | solution.py:209
  193.0 1.3 collective-permute-start.2
  194.3 1.2 collective-permute-start.3
  195.5 0.3 collective-permute-start.5
  196.0 23.8 %all-to-all-done = bf16[16,96,256]{2,1,0:T(8,128)(2,1)S(1)} async-done(((bf16[16,96,256]{2,1,0:T(8,128)(2,1)}), bf16[16,96,256]{2,1,0:T(8,128)(2,1)S(1)}, u32[]{:S(2)}, u32[]{:S(2)}) %all-to-all-start) | async-done | bytes 786464 | tf_op jit(solution)/shard_map/all_to_all | solution.py:209
  219.8 3.9 fusion.39
  223.7 0.3 multiply_reduce_fusion.2
  224.0 0.3 add_convert_fusion.3
  224.4 0.3 collective-permute-start
  225.3 0.6 pad_maximum_fusion.5.bias_ref
  225.9 1.3 collective-permute-done
  227.2 1.3 pad_maximum_fusion.rows_ref
  228.4 17.4 %collective-permute-done.2.refs_3_ = bf16[768,1536]{1,0:T(8,128)(2,1)} collective-permute-done((bf16[768,1536]{1,0:T(8,128)(2,1)}, bf16[768,1536]{1,0:T(8,128)(2,1)}, u32[]{:S(2)}, u32[]{:S(2)}) %collective-permute-start.2) | collective-permute-done | bytes 2359328 | tf_op jit(solution)/shard_map/ppermute | solution.py:159
  245.8 0.9 collective-permute-done.3.refs_4_
  246.7 50.6 %collective-permute-done.5.refs_6_ = bf16[768,1536]{1,0:T(8,128)(2,1)} collective-permute-done((bf16[768,1536]{1,0:T(8,128)(2,1)}, bf16[768,1536]{1,0:T(8,128)(2,1)}, u32[]{:S(2)}, u32[]{:S(2)}) %collective-permute-start.5) | collective-permute-done | bytes 2359328 | tf_op jit(solution)/shard_map/ppermute | solution.py:159
  297.3 17.1 %mlp.2 = (f32[256,1536]{1,0:T(8,128)}, f32[256,1536]{1,0:T(8,128)}) custom-call(bf16[512,1536]{1,0:T(8,128)(2,1)} %pad_maximum_fusion.rows_ref, f32[4,1,768]{2,1,0:T(1,128)} %pad_maximum_fusion.5.bias_ref, bf16[768,1536]{1,0:T(8,128)(2,1)} %bitcast.11.refs_0_, bf16[768,1536]{1,0:T(8,128)(2,1)} %bitcast.12.refs_1_, ...), custom_call_target="tpu_custom_call" | custom-call | flops 9663676416 | bytes 18874368 | tf_op jit(solution)/shard_map/mlp/pallas_call | solution.py:133
  314.4 1.6 collective-permute-start.7
  316.0 3.2 collective-permute-done.7
  319.3 1.8 fusion.35
  321.1 0.3 multiply_reduce_fusion.1
  321.4 1.2 add_convert_fusion.2
  322.8 0.6 all-gather.21.cloned.1.call-update
  323.4 5.0 constant_dynamic-slice_fusion.4
  328.4 0.3 collective-permute-start.9
  328.7 1.2 collective-permute-start.12
  329.9 63.8 %all-gather.17.cloned.1.call-done = bf16[4096,1536]{1,0:T(8,128)(2,1)} async-done(((bf16[256,1536]{1,0:T(8,128)(2,1)}), bf16[4096,1536]{1,0:T(8,128)(2,1)}) %all-gather.17.cloned.1.call-update) | async-done | bytes 12582928 | tf_op jit(solution)/shard_map/all_gather | solution.py:206
  393.6 21.4 %attention.3 = bf16[16,96,256]{2,1,0:T(8,128)(2,1)} custom-call(bf16[16,256,1536]{2,1,0:T(8,128)(2,1)} %bitcast.82, bf16[288,1536]{1,0:T(8,128)(2,1)} %bitcast.75), custom_call_target="tpu_custom_call" | custom-call | flops 10066329600 | bytes 12582912 | tf_op jit(solution)/shard_map/attention/pallas_call | solution.py:76
  415.0 6.4 %all-to-all-start.1 = ((bf16[16,96,256]{2,1,0:T(8,128)(2,1)}), bf16[16,96,256]{2,1,0:T(8,128)(2,1)S(1)}, u32[]{:S(2)}, u32[]{:S(2)}) async-start(bf16[16,96,256]{2,1,0:T(8,128)(2,1)} %attention.3), calls=%async_computation.1 | async-start | bytes 1572864 | tf_op jit(solution)/shard_map/all_to_all | solution.py:209
  421.4 1.2 collective-permute-start.10
  422.6 1.2 collective-permute-start.11
  423.8 0.3 collective-permute-start.13
  424.4 24.1 %all-gather.21.cloned.1.call-done = bf16[1,1,1536,1536]{3,2,1,0:T(8,128)(2,1)} async-done(((bf16[1,1,96,1536]{3,2,1,0:T(8,128)(2,1)}), bf16[1,1,1536,1536]{3,2,1,0:T(8,128)(2,1)}) %all-gather.21.cloned.1.call-update) | async-done | bytes 4718608 | tf_op jit(solution)/shard_map/all_gather | solution.py:213
  448.4 0.9 copy-done.2
  449.3 4.1 fusion.40
  453.4 0.3 multiply_reduce_fusion
  453.7 0.3 add_convert_fusion.1
  454.1 0.6 collective-permute-start.8
  455.0 0.6 pad_maximum_fusion.6.bias_ref
  455.6 1.1 collective-permute-done.8
  456.7 1.3 pad_maximum_fusion.1.rows_ref
  457.9 16.2 %collective-permute-done.10.refs_3_ = bf16[768,1536]{1,0:T(8,128)(2,1)} collective-permute-done((bf16[768,1536]{1,0:T(8,128)(2,1)}, bf16[768,1536]{1,0:T(8,128)(2,1)}, u32[]{:S(2)}, u32[]{:S(2)}) %collective-permute-start.10) | collective-permute-done | bytes 2359328 | tf_op jit(solution)/shard_map/ppermute | solution.py:159
  474.2 0.9 collective-permute-done.11.refs_4_
  475.1 50.6 %collective-permute-done.13.refs_6_ = bf16[768,1536]{1,0:T(8,128)(2,1)} collective-permute-done((bf16[768,1536]{1,0:T(8,128)(2,1)}, bf16[768,1536]{1,0:T(8,128)(2,1)}, u32[]{:S(2)}, u32[]{:S(2)}) %collective-permute-start.13) | collective-permute-done | bytes 2359328 | tf_op jit(solution)/shard_map/ppermute | solution.py:159
  525.6 17.1 %mlp.3 = (f32[256,1536]{1,0:T(8,128)}, f32[256,1536]{1,0:T(8,128)}) custom-call(bf16[512,1536]{1,0:T(8,128)(2,1)} %pad_maximum_fusion.1.rows_ref, f32[4,1,768]{2,1,0:T(1,128)} %pad_maximum_fusion.6.bias_ref, bf16[768,1536]{1,0:T(8,128)(2,1)} %bitcast.20.refs_0_, bf16[768,1536]{1,0:T(8,128)(2,1)} %bitcast.21.refs_1_, ...), custom_call_target="tpu_custom_call" | custom-call | flops 9663676416 | bytes 18874368 | tf_op jit(solution)/shard_map/mlp/pallas_call | solution.py:133
  542.8 1.6 collective-permute-start.15
  544.4 3.2 collective-permute-done.15
  547.7 2.8 fusion.26
  (67 shorter events, 2.7 us)
Async XLA Ops:
  6.5 63.4 %all-gather.15.cloned.1.call-start = ((), (), s32[]{:S(2)}) async-start(), calls=%async_computation.3 | async-start | bytes 10027008 | tf_op jit(solution)/shard_map/all_gather | solution.py:186
  8.4 2.3 copy-start.10
  8.4 22.1 %copy-start.4 = (f32[2,1536]{1,0:T(2,128)S(1)}, f32[2,1536]{1,0:T(2,128)}, u32[]{:S(2)}) copy-start(f32[2,1536]{1,0:T(2,128)} %param.14) | copy-start | bytes 36868
  8.4 22.1 %copy-start.5 = (f32[2,1536]{1,0:T(2,128)S(1)}, f32[2,1536]{1,0:T(2,128)}, u32[]{:S(2)}) copy-start(f32[2,1536]{1,0:T(2,128)} %param.13) | copy-start | bytes 36868
  9.5 21.0 %copy-start = (bf16[1,256,1536]{2,1,0:T(8,128)(2,1)S(1)}, bf16[1,256,1536]{2,1,0:T(8,128)(2,1)}, u32[]{:S(2)}) copy-start(bf16[1,256,1536]{2,1,0:T(8,128)(2,1)} %param.12) | copy-start | bytes 2359300
  10.5 154.3 %all-gather.13.cloned.1.call-start = ((), (), s32[]{:S(2)}) async-start(), calls=%async_computation.2 | async-start | bytes 18382848 | tf_op jit(solution)/shard_map/all_gather | solution.py:206
  31.1 1.3 copy-start.3
  33.2 1.9 copy-start.1
  34.3 289.1 %all-gather.19.cloned.1.call-start = ((), (), s32[]{:S(2)}) async-start(), calls=%async_computation.5 | async-start | bytes 10027008 | tf_op jit(solution)/shard_map/all_gather | solution.py:186
  74.9 120.6 %collective-permute-start.1 = (bf16[768,1536]{1,0:T(8,128)(2,1)}, bf16[768,1536]{1,0:T(8,128)(2,1)}, u32[]{:S(2)}, u32[]{:S(2)}) collective-permute-start(bf16[768,1536]{1,0:T(8,128)(2,1)} %bitcast.11.refs_0_), channel_id=1, source_target_pairs={{0,16},{16,0},{32,48},{48,32},{1,17},{17,1},{33,49},{49,33},{2,18}... | collective-permute-start | bytes 7077896 | tf_op jit(solution)/shard_map/ppermute | solution.py:159
  76.1 119.6 %collective-permute-start.4 = (bf16[768,1536]{1,0:T(8,128)(2,1)}, bf16[768,1536]{1,0:T(8,128)(2,1)}, u32[]{:S(2)}, u32[]{:S(2)}) collective-permute-start(bf16[768,1536]{1,0:T(8,128)(2,1)} %bitcast.12.refs_1_), channel_id=1, source_target_pairs={{0,32},{16,48},{32,0},{48,16},{1,33},{17,49},{33,1},{49,17},{2,34}... | collective-permute-start | bytes 7077896 | tf_op jit(solution)/shard_map/ppermute | solution.py:159
  186.1 6.7 %copy-start.6 = (f32[2,1536]{1,0:T(2,128)S(1)}, f32[2,1536]{1,0:T(2,128)}, u32[]{:S(2)}) copy-start(f32[2,1536]{1,0:T(2,128)} %param.19) | copy-start | bytes 36868
  186.2 6.7 %copy-start.7 = (f32[2,1536]{1,0:T(2,128)S(1)}, f32[2,1536]{1,0:T(2,128)}, u32[]{:S(2)}) copy-start(f32[2,1536]{1,0:T(2,128)} %param.16) | copy-start | bytes 36868
  186.2 6.7 %copy-start.8 = (f32[2,1536]{1,0:T(2,128)S(1)}, f32[2,1536]{1,0:T(2,128)}, u32[]{:S(2)}) copy-start(f32[2,1536]{1,0:T(2,128)} %param.15) | copy-start | bytes 36868
  186.2 33.6 %all-to-all-start = ((bf16[16,96,256]{2,1,0:T(8,128)(2,1)}), bf16[16,96,256]{2,1,0:T(8,128)(2,1)S(1)}, u32[]{:S(2)}, u32[]{:S(2)}) async-start(bf16[16,96,256]{2,1,0:T(8,128)(2,1)} %attention.2), calls=%async_computation | async-start | bytes 1572864 | tf_op jit(solution)/shard_map/all_to_all | solution.py:209
  192.8 200.9 %all-gather.17.cloned.1.call-start = ((), (), s32[]{:S(2)}) async-start(), calls=%async_computation.4 | async-start | bytes 13369344 | tf_op jit(solution)/shard_map/all_gather | solution.py:206
  193.0 52.8 %collective-permute-start.2 = (bf16[768,1536]{1,0:T(8,128)(2,1)}, bf16[768,1536]{1,0:T(8,128)(2,1)}, u32[]{:S(2)}, u32[]{:S(2)}) collective-permute-start(bf16[768,1536]{1,0:T(8,128)(2,1)} %bitcast.12.refs_1_), channel_id=1, source_target_pairs={{0,16},{16,0},{32,48},{48,32},{1,17},{17,1},{33,49},{49,33},{2,18}... | collective-permute-start | bytes 7077896 | tf_op jit(solution)/shard_map/ppermute | solution.py:159
  194.3 52.4 %collective-permute-start.3 = (bf16[768,1536]{1,0:T(8,128)(2,1)}, bf16[768,1536]{1,0:T(8,128)(2,1)}, u32[]{:S(2)}, u32[]{:S(2)}) collective-permute-start(bf16[768,1536]{1,0:T(8,128)(2,1)} %bitcast.11.refs_0_), channel_id=1, source_target_pairs={{0,32},{16,48},{32,0},{48,16},{1,33},{17,49},{33,1},{49,17},{2,34}... | collective-permute-start | bytes 7077896 | tf_op jit(solution)/shard_map/ppermute | solution.py:159
  195.5 101.8 %collective-permute-start.5 = (bf16[768,1536]{1,0:T(8,128)(2,1)}, bf16[768,1536]{1,0:T(8,128)(2,1)}, u32[]{:S(2)}, u32[]{:S(2)}) collective-permute-start(bf16[768,1536]{1,0:T(8,128)(2,1)} %collective-permute-done.1.refs_2_), channel_id=1, source_target_pairs={{0,32},{16,48},{32,0},{48,16},{1,33},{17,49},{33,1},{49,17},{2,34}... | collective-permute-start | bytes 7077896 | tf_op jit(solution)/shard_map/ppermute | solution.py:159
  195.8 101.5 %collective-permute-start.6 = (bf16[768,1536]{1,0:T(8,128)(2,1)}, bf16[768,1536]{1,0:T(8,128)(2,1)}, u32[]{:S(2)}, u32[]{:S(2)}) collective-permute-start(bf16[768,1536]{1,0:T(8,128)(2,1)} %collective-permute-done.4.refs_5_), channel_id=1, source_target_pairs={{0,16},{16,0},{32,48},{48,32},{1,17},{17,1},{33,49},{49,33},{2,18}... | collective-permute-start | bytes 7077896 | tf_op jit(solution)/shard_map/ppermute | solution.py:159
  224.4 2.8 collective-permute-start
  228.4 87.6 %copy-start.9 = (f32[2,1536]{1,0:T(2,128)S(1)}, f32[2,1536]{1,0:T(2,128)}, u32[]{:S(2)}) copy-start(f32[2,1536]{1,0:T(2,128)} %param.23) | copy-start | bytes 36868
  314.4 4.9 collective-permute-start.7
  322.7 125.7 %all-gather.21.cloned.1.call-start = ((), (), s32[]{:S(2)}) async-start(), calls=%async_computation.6 | async-start | bytes 5013504 | tf_op jit(solution)/shard_map/all_gather | solution.py:213
  328.4 95.4 %collective-permute-start.9 = (bf16[768,1536]{1,0:T(8,128)(2,1)}, bf16[768,1536]{1,0:T(8,128)(2,1)}, u32[]{:S(2)}, u32[]{:S(2)}) collective-permute-start(bf16[768,1536]{1,0:T(8,128)(2,1)} %bitcast.20.refs_0_), channel_id=1, source_target_pairs={{0,16},{16,0},{32,48},{48,32},{1,17},{17,1},{33,49},{49,33},{2,18}... | collective-permute-start | bytes 7077896 | tf_op jit(solution)/shard_map/ppermute | solution.py:159
  328.7 95.4 %collective-permute-start.12 = (bf16[768,1536]{1,0:T(8,128)(2,1)}, bf16[768,1536]{1,0:T(8,128)(2,1)}, u32[]{:S(2)}, u32[]{:S(2)}) collective-permute-start(bf16[768,1536]{1,0:T(8,128)(2,1)} %bitcast.21.refs_1_), channel_id=1, source_target_pairs={{0,32},{16,48},{32,0},{48,16},{1,33},{17,49},{33,1},{49,17},{2,34}... | collective-permute-start | bytes 7077896 | tf_op jit(solution)/shard_map/ppermute | solution.py:159
  415.0 33.4 %all-to-all-start.1 = ((bf16[16,96,256]{2,1,0:T(8,128)(2,1)}), bf16[16,96,256]{2,1,0:T(8,128)(2,1)S(1)}, u32[]{:S(2)}, u32[]{:S(2)}) async-start(bf16[16,96,256]{2,1,0:T(8,128)(2,1)} %attention.3), calls=%async_computation.1 | async-start | bytes 1572864 | tf_op jit(solution)/shard_map/all_to_all | solution.py:209
  421.4 52.7 %collective-permute-start.10 = (bf16[768,1536]{1,0:T(8,128)(2,1)}, bf16[768,1536]{1,0:T(8,128)(2,1)}, u32[]{:S(2)}, u32[]{:S(2)}) collective-permute-start(bf16[768,1536]{1,0:T(8,128)(2,1)} %bitcast.21.refs_1_), channel_id=1, source_target_pairs={{0,16},{16,0},{32,48},{48,32},{1,17},{17,1},{33,49},{49,33},{2,18}... | collective-permute-start | bytes 7077896 | tf_op jit(solution)/shard_map/ppermute | solution.py:159
  422.6 52.4 %collective-permute-start.11 = (bf16[768,1536]{1,0:T(8,128)(2,1)}, bf16[768,1536]{1,0:T(8,128)(2,1)}, u32[]{:S(2)}, u32[]{:S(2)}) collective-permute-start(bf16[768,1536]{1,0:T(8,128)(2,1)} %bitcast.20.refs_0_), channel_id=1, source_target_pairs={{0,32},{16,48},{32,0},{48,16},{1,33},{17,49},{33,1},{49,17},{2,34}... | collective-permute-start | bytes 7077896 | tf_op jit(solution)/shard_map/ppermute | solution.py:159
  423.8 101.8 %collective-permute-start.13 = (bf16[768,1536]{1,0:T(8,128)(2,1)}, bf16[768,1536]{1,0:T(8,128)(2,1)}, u32[]{:S(2)}, u32[]{:S(2)}) collective-permute-start(bf16[768,1536]{1,0:T(8,128)(2,1)} %collective-permute-done.9.refs_2_), channel_id=1, source_target_pairs={{0,32},{16,48},{32,0},{48,16},{1,33},{17,49},{33,1},{49,17},{2,34}... | collective-permute-start | bytes 7077896 | tf_op jit(solution)/shard_map/ppermute | solution.py:159
  424.1 101.5 %collective-permute-start.14 = (bf16[768,1536]{1,0:T(8,128)(2,1)}, bf16[768,1536]{1,0:T(8,128)(2,1)}, u32[]{:S(2)}, u32[]{:S(2)}) collective-permute-start(bf16[768,1536]{1,0:T(8,128)(2,1)} %collective-permute-done.12.refs_5_), channel_id=1, source_target_pairs={{0,16},{16,0},{32,48},{48,32},{1,17},{17,1},{33,49},{49,33},{2,18}... | collective-permute-start | bytes 7077896 | tf_op jit(solution)/shard_map/ppermute | solution.py:159
  448.4 0.9 copy-start.2
  454.1 2.6 collective-permute-start.8
  542.8 4.9 collective-permute-start.15
Sparse Core Ops, SparseCore 0:
  10.6 59.3 all-gather.14
  71.6 93.0 all-gather.12
  166.4 73.0 all-gather.18
  322.8 70.7 all-gather.16
  395.1 53.2 all-gather.20

commit v2 on v1

--- a/solution.py
+++ b/solution.py
@@ -148,6 +148,85 @@
     )(both, bias, *[x for up, _, down in weights for x in (up, down)])
 
 
+def lift_kernel(parts, rows_ref, bias_ref, *refs):
+    weights, (act_ref, up_all, turned, sems) = refs[:parts], refs[parts:]
+    units = up_all.shape[0] // parts
+
+    def fetch(m, source):
+        return pltpu.make_async_copy(weights[source], up_all.at[pl.ds(pl.multiple_of(m * units, 16), units)], sems.at[m])
+
+    for m in range(parts):
+        fetch(m, m).start()
+    turned[...] = rows_ref[...].T
+
+    def lift(m, carry):
+        fetch(m, 0).wait()
+        here = pl.ds(pl.multiple_of(m * units, 16), units)
+        pre_act = jnp.dot(up_all[here, :], turned[...], preferred_element_type=F32) + bias_ref[m].T
+        act_ref[here, :] = jax.nn.gelu(pre_act, approximate=True).astype(BF16)
+        return carry
+
+    lax.fori_loop(0, parts, lift, 0)
+
+
+def lower_kernel(parts, act_ref, *refs):
+    weights, (own_ref, other_ref, down_all, sems) = refs[:parts], refs[parts:]
+    half, width = own_ref.shape
+    units = down_all.shape[0] // parts
+    tile = math.gcd(width, 4 * LANES)
+
+    def fetch(n, m):
+        columns = pl.ds(pl.multiple_of(n * tile, tile), tile)
+        return pltpu.make_async_copy(weights[m].at[:, columns], down_all.at[pl.ds(m * units, units), columns], sems.at[n, m])
+
+    for n in range(width // tile):
+        for m in range(parts):
+            fetch(n, m).start()
+
+    def lower(n, carry):
+        for m in range(parts):
+            fetch(n, m).wait()
+        columns = pl.ds(pl.multiple_of(n * tile, tile), tile)
+        result = lax.dot_general(act_ref[...], down_all[:, columns], (((0,), (0,)), ((), ())), preferred_element_type=F32)
+        own_ref[:, columns] = result[:half]
+        other_ref[:, columns] = result[half:]
+        return carry
+
+    lax.fori_loop(0, width // tile, lower, 0)
+
+
+def mlp_lift(both, weights):
+    rows, width = both.shape
+    units, parts = weights[0][0].shape[0], len(weights)
+    whole, far = pl.BlockSpec(memory_space=pltpu.VMEM), pl.BlockSpec(memory_space=pl.ANY)
+    return pl.pallas_call(
+        functools.partial(lift_kernel, parts),
+        out_shape=jax.ShapeDtypeStruct((parts * units, rows), BF16),
+        in_specs=[whole] * 2 + [far] * parts,
+        out_specs=whole,
+        scratch_shapes=[pltpu.VMEM((parts * units, width), BF16), pltpu.VMEM((width, rows), BF16), pltpu.SemaphoreType.DMA((parts,))],
+        cost_estimate=pl.CostEstimate(flops=2 * rows * width * units * parts, bytes_accessed=2 * units * width * parts, transcendentals=rows * units * parts),
+        compiler_params=pltpu.CompilerParams(vmem_limit_bytes=60 * 1024 * 1024),
+        name="mlp_lift",
+    )(both, jnp.stack([bias[None] for _, bias, _ in weights]), *[up for up, _, _ in weights])
+
+
+def mlp_lower(act, weights):
+    rows = act.shape[1]
+    (units, width), parts = weights[0][2].shape, len(weights)
+    whole, far = pl.BlockSpec(memory_space=pltpu.VMEM), pl.BlockSpec(memory_space=pl.ANY)
+    return pl.pallas_call(
+        functools.partial(lower_kernel, parts),
+        out_shape=[jax.ShapeDtypeStruct((rows // 2, width), F32)] * 2,
+        in_specs=[whole] + [far] * parts,
+        out_specs=[whole, whole],
+        scratch_shapes=[pltpu.VMEM((parts * units, width), BF16), pltpu.SemaphoreType.DMA((width // math.gcd(width, 4 * LANES), parts))],
+        cost_estimate=pl.CostEstimate(flops=2 * rows * width * units * parts, bytes_accessed=2 * units * width * parts, transcendentals=0),
+        compiler_params=pltpu.CompilerParams(vmem_limit_bytes=60 * 1024 * 1024),
+        name="mlp_lower",
+    )(act, *[down for _, _, down in weights])
+
+
 def solution(mesh):
     tp_size, dp_size = mesh.shape["tp"], mesh.shape["dp"]
     bits = [1 << n for n in range(dp_size.bit_length() - 1)]
@@ -215,8 +294,13 @@
             resid = resid + (attn + b_out[layer])
             normed_mlp = layer_norm(resid, ln2_gain[layer], ln2_bias[layer])
             both = jnp.concatenate([normed_mlp, partner(normed_mlp)], 0)
-            ahead = mlp_weights(layer + 1, to_pair, normed_mlp) if layer + 1 < layers else None
-            own, other = mlp(both, weights)
+            ahead = None
+            if layer + 1 < layers:
+                act = mlp_lift(both, weights)
+                ahead = mlp_weights(layer + 1, to_pair, act)
+                own, other = mlp_lower(act, weights)
+            else:
+                own, other = mlp(both, weights)
             summed = own + partner(other)
             resid = resid + (summed + b_down[layer])
             weights = ahead

time: 559 us -> 564 us (level)
    pallas_call x0 -> x2, Pallas kernels: none -> 22.6 us  [the longest x1 11.7 us: mlp_lift(): pl.pallas_call(functools.partial(lift_kernel, parts), out_shape=jax.Shape...]
    pallas_call x2 -> x1, Pallas kernels: 34.2 us -> 17.1 us  [mlp(): pl.pallas_call(functools.partial(mlp_kernel, parts), out_shape=[jax.Shape...]
  transfers between devices with their start and end apart: 23 -> 23, of which waited for: 15 -> 14; matrix products, arithmetic and copies ran while one was open for 6% -> 6% of each run, Pallas kernels for 11% -> 12%
where the time goes in v2:
time: 564 us; the launch traced here: 562 us
  waiting for transfers between devices  378 us (67%)
  Pallas kernels  82.5 us (15%)
  starting transfers between devices  28 us (5%)
  blocking collectives  19.8 us (4%)
  local copies, waits for them, and re-layouts  17.2 us (3%)
  other arithmetic  14.9 us (3%)
  between operations  13.5 us (2%)
  matrix products  7.99 us (1%)
    all_gather x2, waiting for transfers between devices, forward(): gathered = lax.all_gather(to_send, 'tp', axis=0)  151 us
    ppermute x12, waiting for transfers between devices, spread(): lax.ppermute(b, 'dp', pairs)  136 us
    pallas_call x2, Pallas kernels, attention(): pl.pallas_call(functools.partial(attention_kernel, 1.0 / math.sqrt(head_d...  42.8 us
    all_gather x2, waiting for transfers between devices, mlp_weights(): pair = lax.all_gather(to_pair, 'tp', axis=0)  33.6 us
    all_gather x1, waiting for transfers between devices, forward(): w_out_all = lax.all_gather(w_out[layer][0], 'tp', axis=0, tiled=True)  24.1 us
    all_to_all x2, waiting for transfers between devices, forward(): heads = lax.all_to_all(heads, 'tp', 0, 0, tiled=True).reshape(-1, share)  23.8 us
    all_gather x1, blocking collectives, forward(): b_up_all = lax.all_gather(b_up, 'tp', axis=0)  19.8 us
    pallas_call x1, Pallas kernels, mlp(): pl.pallas_call(functools.partial(mlp_kernel, parts), out_shape=[jax.Shape...  17.1 us
  transfers between devices with their start and end apart: 23, of which 14 were waited for; matrix products, arithmetic and copies ran while one was open for 6% of the time, Pallas kernels for 12%

profile of v2, /device:TPU:53, one launch (start us, length us, event | category | flops | bytes accessed | tf_op | source)
XLA Modules:
  0.0 562.3 jit_solution(8339699676054306984)
XLA Ops:
  6.6 1.7 constant_dynamic-slice_fusion.13
  8.4 1.1 dynamic-slice_bitcast_fusion
  9.6 0.9 pad_maximum_fusion.4
  10.7 19.8 %all-gather.6 = f32[16,2,384]{2,1,0:T(2,128)S(1)} all-gather(f32[1,2,384]{2,1,0:T(2,128)S(1)} %bitcast.79), channel_id=2, replica_groups=mesh['dp'=4,'tp'=16] {'tp'}, dimensions={0}, use_global_device_ids=true | all-gather | bytes 52224 | tf_op jit(solution)/shard_map/all_gather | solution.py:255
  30.8 0.3 fusion.22
  31.2 0.9 pad_maximum_fusion.3
  32.0 0.4 fusion.25
  32.4 0.7 fusion.37
  33.2 1.1 pad_maximum_fusion.2
  34.4 0.7 all-gather.19.cloned.1.call-update
  35.1 1.3 fusion.36
  36.4 33.5 %all-gather.15.cloned.1.call-done = bf16[3072,1536]{1,0:T(8,128)(2,1)} async-done(((bf16[192,1536]{1,0:T(8,128)(2,1)}), bf16[3072,1536]{1,0:T(8,128)(2,1)}) %all-gather.15.cloned.1.call-update) | async-done | bytes 9437200 | tf_op jit(solution)/shard_map/all_gather | solution.py:265
  70.0 4.9 constant_dynamic-slice_fusion.11
  74.9 1.2 collective-permute-start.1
  76.1 1.2 collective-permute-start.5
  77.3 87.4 %all-gather.13.cloned.1.call-done = bf16[5632,1536]{1,0:T(8,128)(2,1)} async-done(((bf16[352,1536]{1,0:T(8,128)(2,1)}), bf16[5632,1536]{1,0:T(8,128)(2,1)}) %all-gather.13.cloned.1.call-update) | async-done | bytes 17301520 | tf_op jit(solution)/shard_map/all_gather | solution.py:285
  164.7 21.4 %attention.2 = bf16[16,96,256]{2,1,0:T(8,128)(2,1)} custom-call(bf16[16,352,1536]{2,1,0:T(8,128)(2,1)} %bitcast.80, bf16[288,1536]{1,0:T(8,128)(2,1)} %bitcast.76), custom_call_target="tpu_custom_call" | custom-call | flops 10066329600 | bytes 12582912 | tf_op jit(solution)/shard_map/attention/pallas_call | solution.py:76
  186.2 6.6 %all-to-all-start = ((bf16[16,96,256]{2,1,0:T(8,128)(2,1)}), bf16[16,96,256]{2,1,0:T(8,128)(2,1)S(1)}, u32[]{:S(2)}, u32[]{:S(2)}) async-start(bf16[16,96,256]{2,1,0:T(8,128)(2,1)} %attention.2), calls=%async_computation | async-start | bytes 1572864 | tf_op jit(solution)/shard_map/all_to_all | solution.py:288
  193.0 1.3 collective-permute-start.2
  194.3 1.2 collective-permute-start.4
  195.5 0.3 collective-permute-start.3
  196.0 23.8 %all-to-all-done = bf16[16,96,256]{2,1,0:T(8,128)(2,1)S(1)} async-done(((bf16[16,96,256]{2,1,0:T(8,128)(2,1)}), bf16[16,96,256]{2,1,0:T(8,128)(2,1)S(1)}, u32[]{:S(2)}, u32[]{:S(2)}) %all-to-all-start) | async-done | bytes 786464 | tf_op jit(solution)/shard_map/all_to_all | solution.py:288
  219.8 3.9 fusion.39
  223.7 0.3 multiply_reduce_fusion.2
  224.0 0.3 add_convert_fusion.3
  224.4 0.3 collective-permute-start
  225.3 0.6 pad_maximum_fusion.5.bias_ref
  225.9 1.3 collective-permute-done
  227.2 1.2 pad_maximum_fusion.rows_ref
  228.4 17.4 %collective-permute-done.2.refs_2_ = bf16[768,1536]{1,0:T(8,128)(2,1)} collective-permute-done((bf16[768,1536]{1,0:T(8,128)(2,1)}, bf16[768,1536]{1,0:T(8,128)(2,1)}, u32[]{:S(2)}, u32[]{:S(2)}) %collective-permute-start.2) | collective-permute-done | bytes 2359328 | tf_op jit(solution)/shard_map/ppermute | solution.py:238
  245.8 50.6 %collective-permute-done.3.refs_3_ = bf16[768,1536]{1,0:T(8,128)(2,1)} collective-permute-done((bf16[768,1536]{1,0:T(8,128)(2,1)}, bf16[768,1536]{1,0:T(8,128)(2,1)}, u32[]{:S(2)}, u32[]{:S(2)}) %collective-permute-start.3) | collective-permute-done | bytes 2359328 | tf_op jit(solution)/shard_map/ppermute | solution.py:238
  296.4 11.7 %mlp_lift.1.act_ref = bf16[3072,512]{1,0:T(8,128)(2,1)} custom-call(bf16[512,1536]{1,0:T(8,128)(2,1)} %pad_maximum_fusion.rows_ref, f32[4,1,768]{2,1,0:T(1,128)} %pad_maximum_fusion.5.bias_ref, bf16[768,1536]{1,0:T(8,128)(2,1)} %bitcast.11.refs_0_, bf16[768,1536]{1,0:T(8,128)(2,1)} %collective-permute-done.1.refs_1_, ...), custom_call_target="tpu_custom_call" | custom-call | flops 4831838208 | bytes 9437184 | tf_op jit(solution)/shard_map/mlp_lift/pallas_call | solution.py:202
  308.1 10.9 %mlp_lower.1 = (f32[256,1536]{1,0:T(8,128)}, f32[256,1536]{1,0:T(8,128)}) custom-call(bf16[3072,512]{1,0:T(8,128)(2,1)} %mlp_lift.1.act_ref, bf16[768,1536]{1,0:T(8,128)(2,1)} %bitcast.12.refs_0_, bf16[768,1536]{1,0:T(8,128)(2,1)} %collective-permute-done.4.refs_1_, bf16[768,1536]{1,0:T(8,128)(2,1)} %collective-permute-done.5.refs_2_, ...), custom_call_target="tpu_custom_call" | custom-call | flops 4831838208 | bytes 9437184 | tf_op jit(solution)/shard_map/mlp_lower/pallas_call | solution.py:218
  319.0 1.4 collective-permute-start.7
  320.4 3.2 collective-permute-done.7
  323.6 1.8 fusion.35
  325.4 0.3 multiply_reduce_fusion.1
  325.8 1.2 add_convert_fusion.2
  327.1 0.6 all-gather.21.cloned.1.call-update
  327.7 5.0 constant_dynamic-slice_fusion.4
  332.8 1.2 collective-permute-start.9
  334.0 1.2 collective-permute-start.12
  335.2 63.7 %all-gather.17.cloned.1.call-done = bf16[4096,1536]{1,0:T(8,128)(2,1)} async-done(((bf16[256,1536]{1,0:T(8,128)(2,1)}), bf16[4096,1536]{1,0:T(8,128)(2,1)}) %all-gather.17.cloned.1.call-update) | async-done | bytes 12582928 | tf_op jit(solution)/shard_map/all_gather | solution.py:285
  398.9 21.4 %attention.3 = bf16[16,96,256]{2,1,0:T(8,128)(2,1)} custom-call(bf16[16,256,1536]{2,1,0:T(8,128)(2,1)} %bitcast.82, bf16[288,1536]{1,0:T(8,128)(2,1)} %bitcast.75), custom_call_target="tpu_custom_call" | custom-call | flops 10066329600 | bytes 12582912 | tf_op jit(solution)/shard_map/attention/pallas_call | solution.py:76
  420.3 6.4 %all-to-all-start.1 = ((bf16[16,96,256]{2,1,0:T(8,128)(2,1)}), bf16[16,96,256]{2,1,0:T(8,128)(2,1)S(1)}, u32[]{:S(2)}, u32[]{:S(2)}) async-start(bf16[16,96,256]{2,1,0:T(8,128)(2,1)} %attention.3), calls=%async_computation.1 | async-start | bytes 1572864 | tf_op jit(solution)/shard_map/all_to_all | solution.py:288
  426.7 1.2 collective-permute-start.10
  427.9 1.2 collective-permute-start.11
  429.1 0.3 collective-permute-start.13
  429.7 24.1 %all-gather.21.cloned.1.call-done = bf16[1,1,1536,1536]{3,2,1,0:T(8,128)(2,1)} async-done(((bf16[1,1,96,1536]{3,2,1,0:T(8,128)(2,1)}), bf16[1,1,1536,1536]{3,2,1,0:T(8,128)(2,1)}) %all-gather.21.cloned.1.call-update) | async-done | bytes 4718608 | tf_op jit(solution)/shard_map/all_gather | solution.py:292
  453.7 0.9 copy-done.2
  454.6 4.1 fusion.40
  458.7 0.3 multiply_reduce_fusion
  459.0 0.3 add_convert_fusion.1
  459.3 0.6 collective-permute-start.8
  460.3 0.6 pad_maximum_fusion.6.bias_ref
  460.9 1.1 collective-permute-done.8
  462.0 1.3 pad_maximum_fusion.1.rows_ref
  463.2 16.2 %collective-permute-done.10.refs_3_ = bf16[768,1536]{1,0:T(8,128)(2,1)} collective-permute-done((bf16[768,1536]{1,0:T(8,128)(2,1)}, bf16[768,1536]{1,0:T(8,128)(2,1)}, u32[]{:S(2)}, u32[]{:S(2)}) %collective-permute-start.10) | collective-permute-done | bytes 2359328 | tf_op jit(solution)/shard_map/ppermute | solution.py:238
  479.4 0.9 collective-permute-done.11.refs_4_
  480.4 50.6 %collective-permute-done.13.refs_6_ = bf16[768,1536]{1,0:T(8,128)(2,1)} collective-permute-done((bf16[768,1536]{1,0:T(8,128)(2,1)}, bf16[768,1536]{1,0:T(8,128)(2,1)}, u32[]{:S(2)}, u32[]{:S(2)}) %collective-permute-start.13) | collective-permute-done | bytes 2359328 | tf_op jit(solution)/shard_map/ppermute | solution.py:238
  530.9 17.1 %mlp.1 = (f32[256,1536]{1,0:T(8,128)}, f32[256,1536]{1,0:T(8,128)}) custom-call(bf16[512,1536]{1,0:T(8,128)(2,1)} %pad_maximum_fusion.1.rows_ref, f32[4,1,768]{2,1,0:T(1,128)} %pad_maximum_fusion.6.bias_ref, bf16[768,1536]{1,0:T(8,128)(2,1)} %bitcast.20.refs_0_, bf16[768,1536]{1,0:T(8,128)(2,1)} %bitcast.21.refs_1_, ...), custom_call_target="tpu_custom_call" | custom-call | flops 9663676416 | bytes 18874368 | tf_op jit(solution)/shard_map/mlp/pallas_call | solution.py:133
  548.1 1.6 collective-permute-start.15
  549.7 3.2 collective-permute-done.15
  553.0 2.8 fusion.26
  (68 shorter events, 2.7 us)
Async XLA Ops:
  6.5 63.4 %all-gather.15.cloned.1.call-start = ((), (), s32[]{:S(2)}) async-start(), calls=%async_computation.3 | async-start | bytes 10027008 | tf_op jit(solution)/shard_map/all_gather | solution.py:265
  8.4 2.3 copy-start.10
  8.4 22.1 %copy-start.4 = (f32[2,1536]{1,0:T(2,128)S(1)}, f32[2,1536]{1,0:T(2,128)}, u32[]{:S(2)}) copy-start(f32[2,1536]{1,0:T(2,128)} %param.14) | copy-start | bytes 36868
  8.4 22.1 %copy-start.5 = (f32[2,1536]{1,0:T(2,128)S(1)}, f32[2,1536]{1,0:T(2,128)}, u32[]{:S(2)}) copy-start(f32[2,1536]{1,0:T(2,128)} %param.13) | copy-start | bytes 36868
  9.5 21.0 %copy-start = (bf16[1,256,1536]{2,1,0:T(8,128)(2,1)S(1)}, bf16[1,256,1536]{2,1,0:T(8,128)(2,1)}, u32[]{:S(2)}) copy-start(bf16[1,256,1536]{2,1,0:T(8,128)(2,1)} %param.12) | copy-start | bytes 2359300
  10.5 154.3 %all-gather.13.cloned.1.call-start = ((), (), s32[]{:S(2)}) async-start(), calls=%async_computation.2 | async-start | bytes 18382848 | tf_op jit(solution)/shard_map/all_gather | solution.py:285
  31.1 1.3 copy-start.3
  33.2 1.9 copy-start.1
  34.3 293.4 %all-gather.19.cloned.1.call-start = ((), (), s32[]{:S(2)}) async-start(), calls=%async_computation.5 | async-start | bytes 10027008 | tf_op jit(solution)/shard_map/all_gather | solution.py:265
  74.9 120.6 %collective-permute-start.1 = (bf16[768,1536]{1,0:T(8,128)(2,1)}, bf16[768,1536]{1,0:T(8,128)(2,1)}, u32[]{:S(2)}, u32[]{:S(2)}) collective-permute-start(bf16[768,1536]{1,0:T(8,128)(2,1)} %bitcast.11.refs_0_), channel_id=1, source_target_pairs={{0,16},{16,0},{32,48},{48,32},{1,17},{17,1},{33,49},{49,33},{2,18}... | collective-permute-start | bytes 7077896 | tf_op jit(solution)/shard_map/ppermute | solution.py:238
  76.1 119.6 %collective-permute-start.5 = (bf16[768,1536]{1,0:T(8,128)(2,1)}, bf16[768,1536]{1,0:T(8,128)(2,1)}, u32[]{:S(2)}, u32[]{:S(2)}) collective-permute-start(bf16[768,1536]{1,0:T(8,128)(2,1)} %bitcast.12.refs_0_), channel_id=1, source_target_pairs={{0,32},{16,48},{32,0},{48,16},{1,33},{17,49},{33,1},{49,17},{2,34}... | collective-permute-start | bytes 7077896 | tf_op jit(solution)/shard_map/ppermute | solution.py:238
  186.1 6.7 %copy-start.6 = (f32[2,1536]{1,0:T(2,128)S(1)}, f32[2,1536]{1,0:T(2,128)}, u32[]{:S(2)}) copy-start(f32[2,1536]{1,0:T(2,128)} %param.19) | copy-start | bytes 36868
  186.2 6.7 %copy-start.7 = (f32[2,1536]{1,0:T(2,128)S(1)}, f32[2,1536]{1,0:T(2,128)}, u32[]{:S(2)}) copy-start(f32[2,1536]{1,0:T(2,128)} %param.16) | copy-start | bytes 36868
  186.2 6.7 %copy-start.8 = (f32[2,1536]{1,0:T(2,128)S(1)}, f32[2,1536]{1,0:T(2,128)}, u32[]{:S(2)}) copy-start(f32[2,1536]{1,0:T(2,128)} %param.15) | copy-start | bytes 36868
  186.2 33.6 %all-to-all-start = ((bf16[16,96,256]{2,1,0:T(8,128)(2,1)}), bf16[16,96,256]{2,1,0:T(8,128)(2,1)S(1)}, u32[]{:S(2)}, u32[]{:S(2)}) async-start(bf16[16,96,256]{2,1,0:T(8,128)(2,1)} %attention.2), calls=%async_computation | async-start | bytes 1572864 | tf_op jit(solution)/shard_map/all_to_all | solution.py:288
  192.8 206.2 %all-gather.17.cloned.1.call-start = ((), (), s32[]{:S(2)}) async-start(), calls=%async_computation.4 | async-start | bytes 13369344 | tf_op jit(solution)/shard_map/all_gather | solution.py:285
  193.0 52.8 %collective-permute-start.2 = (bf16[768,1536]{1,0:T(8,128)(2,1)}, bf16[768,1536]{1,0:T(8,128)(2,1)}, u32[]{:S(2)}, u32[]{:S(2)}) collective-permute-start(bf16[768,1536]{1,0:T(8,128)(2,1)} %bitcast.11.refs_0_), channel_id=1, source_target_pairs={{0,32},{16,48},{32,0},{48,16},{1,33},{17,49},{33,1},{49,17},{2,34}... | collective-permute-start | bytes 7077896 | tf_op jit(solution)/shard_map/ppermute | solution.py:238
  194.3 113.8 %collective-permute-start.4 = (bf16[768,1536]{1,0:T(8,128)(2,1)}, bf16[768,1536]{1,0:T(8,128)(2,1)}, u32[]{:S(2)}, u32[]{:S(2)}) collective-permute-start(bf16[768,1536]{1,0:T(8,128)(2,1)} %bitcast.12.refs_0_), channel_id=1, source_target_pairs={{0,16},{16,0},{32,48},{48,32},{1,17},{17,1},{33,49},{49,33},{2,18}... | collective-permute-start | bytes 7077896 | tf_op jit(solution)/shard_map/ppermute | solution.py:238
  195.5 100.9 %collective-permute-start.3 = (bf16[768,1536]{1,0:T(8,128)(2,1)}, bf16[768,1536]{1,0:T(8,128)(2,1)}, u32[]{:S(2)}, u32[]{:S(2)}) collective-permute-start(bf16[768,1536]{1,0:T(8,128)(2,1)} %collective-permute-done.1.refs_1_), channel_id=1, source_target_pairs={{0,32},{16,48},{32,0},{48,16},{1,33},{17,49},{33,1},{49,17},{2,34}... | collective-permute-start | bytes 7077896 | tf_op jit(solution)/shard_map/ppermute | solution.py:238
  195.8 112.3 %collective-permute-start.6 = (bf16[768,1536]{1,0:T(8,128)(2,1)}, bf16[768,1536]{1,0:T(8,128)(2,1)}, u32[]{:S(2)}, u32[]{:S(2)}) collective-permute-start(bf16[768,1536]{1,0:T(8,128)(2,1)} %collective-permute-done.5.refs_2_), channel_id=1, source_target_pairs={{0,16},{16,0},{32,48},{48,32},{1,17},{17,1},{33,49},{49,33},{2,18}... | collective-permute-start | bytes 7077896 | tf_op jit(solution)/shard_map/ppermute | solution.py:238
  224.4 2.8 collective-permute-start
  308.1 12.3 %copy-start.9 = (f32[2,1536]{1,0:T(2,128)S(1)}, f32[2,1536]{1,0:T(2,128)}, u32[]{:S(2)}) copy-start(f32[2,1536]{1,0:T(2,128)} %param.23) | copy-start | bytes 36868
  319.0 4.6 collective-permute-start.7
  327.1 126.7 %all-gather.21.cloned.1.call-start = ((), (), s32[]{:S(2)}) async-start(), calls=%async_computation.6 | async-start | bytes 5013504 | tf_op jit(solution)/shard_map/all_gather | solution.py:292
  332.8 96.3 %collective-permute-start.9 = (bf16[768,1536]{1,0:T(8,128)(2,1)}, bf16[768,1536]{1,0:T(8,128)(2,1)}, u32[]{:S(2)}, u32[]{:S(2)}) collective-permute-start(bf16[768,1536]{1,0:T(8,128)(2,1)} %bitcast.20.refs_0_), channel_id=1, source_target_pairs={{0,16},{16,0},{32,48},{48,32},{1,17},{17,1},{33,49},{49,33},{2,18}... | collective-permute-start | bytes 7077896 | tf_op jit(solution)/shard_map/ppermute | solution.py:238
  334.0 95.4 %collective-permute-start.12 = (bf16[768,1536]{1,0:T(8,128)(2,1)}, bf16[768,1536]{1,0:T(8,128)(2,1)}, u32[]{:S(2)}, u32[]{:S(2)}) collective-permute-start(bf16[768,1536]{1,0:T(8,128)(2,1)} %bitcast.21.refs_1_), channel_id=1, source_target_pairs={{0,32},{16,48},{32,0},{48,16},{1,33},{17,49},{33,1},{49,17},{2,34}... | collective-permute-start | bytes 7077896 | tf_op jit(solution)/shard_map/ppermute | solution.py:238
  420.3 33.4 %all-to-all-start.1 = ((bf16[16,96,256]{2,1,0:T(8,128)(2,1)}), bf16[16,96,256]{2,1,0:T(8,128)(2,1)S(1)}, u32[]{:S(2)}, u32[]{:S(2)}) async-start(bf16[16,96,256]{2,1,0:T(8,128)(2,1)} %attention.3), calls=%async_computation.1 | async-start | bytes 1572864 | tf_op jit(solution)/shard_map/all_to_all | solution.py:288
  426.7 52.7 %collective-permute-start.10 = (bf16[768,1536]{1,0:T(8,128)(2,1)}, bf16[768,1536]{1,0:T(8,128)(2,1)}, u32[]{:S(2)}, u32[]{:S(2)}) collective-permute-start(bf16[768,1536]{1,0:T(8,128)(2,1)} %bitcast.21.refs_1_), channel_id=1, source_target_pairs={{0,16},{16,0},{32,48},{48,32},{1,17},{17,1},{33,49},{49,33},{2,18}... | collective-permute-start | bytes 7077896 | tf_op jit(solution)/shard_map/ppermute | solution.py:238
  427.9 52.4 %collective-permute-start.11 = (bf16[768,1536]{1,0:T(8,128)(2,1)}, bf16[768,1536]{1,0:T(8,128)(2,1)}, u32[]{:S(2)}, u32[]{:S(2)}) collective-permute-start(bf16[768,1536]{1,0:T(8,128)(2,1)} %bitcast.20.refs_0_), channel_id=1, source_target_pairs={{0,32},{16,48},{32,0},{48,16},{1,33},{17,49},{33,1},{49,17},{2,34}... | collective-permute-start | bytes 7077896 | tf_op jit(solution)/shard_map/ppermute | solution.py:238
  429.1 101.8 %collective-permute-start.13 = (bf16[768,1536]{1,0:T(8,128)(2,1)}, bf16[768,1536]{1,0:T(8,128)(2,1)}, u32[]{:S(2)}, u32[]{:S(2)}) collective-permute-start(bf16[768,1536]{1,0:T(8,128)(2,1)} %collective-permute-done.9.refs_2_), channel_id=1, source_target_pairs={{0,32},{16,48},{32,0},{48,16},{1,33},{17,49},{33,1},{49,17},{2,34}... | collective-permute-start | bytes 7077896 | tf_op jit(solution)/shard_map/ppermute | solution.py:238
  429.4 101.5 %collective-permute-start.14 = (bf16[768,1536]{1,0:T(8,128)(2,1)}, bf16[768,1536]{1,0:T(8,128)(2,1)}, u32[]{:S(2)}, u32[]{:S(2)}) collective-permute-start(bf16[768,1536]{1,0:T(8,128)(2,1)} %collective-permute-done.12.refs_5_), channel_id=1, source_target_pairs={{0,16},{16,0},{32,48},{48,32},{1,17},{17,1},{33,49},{49,33},{2,18}... | collective-permute-start | bytes 7077896 | tf_op jit(solution)/shard_map/ppermute | solution.py:238
  453.7 0.9 copy-start.2
  459.3 2.6 collective-permute-start.8
  548.1 4.9 collective-permute-start.15
Sparse Core Ops, SparseCore 0:
  10.6 59.3 all-gather.14
  71.6 93.0 all-gather.12
  166.4 73.0 all-gather.18
  327.2 71.6 all-gather.16
  400.4 53.2 all-gather.20
